TPU v7x, 128 devices: a whole 4x4x4 slice. The times are simulated.
128 devices in a mesh: node: 32 (over x, z, core), local: 4 (over y).
Axes of the slice: x: 4, y: 4, z: 4, core: 2. Of those that a mesh axis runs over, the one named last changes fastest.
Arguments:
- tokens: bfloat16 [8192, 5120], P(('node', 'local')), may hold values from -6 to 6
- node_ids: int32 [8192, 3], P(('node', 'local')), may hold values from 0 to 31, as said below
- expert_ids: int32 [8192, 6], P(('node', 'local')), may hold values from 0 to 95, as said below
- gate_weights: bfloat16 [8192, 6], P(('node', 'local')), may hold values from 0.049804688 to 1
- up_weight: bfloat16 [96, 5120, 1536], P('node', None, 'local'), may hold values from -0.078125 to 0.078125
- down_weight: bfloat16 [96, 1536, 5120], P('node', 'local'), may hold values from -0.15625 to 0.15625
Outputs:
- routed_out: bfloat16 [8192, 5120], P(('node', 'local'))
Inputs may be any that keep to these rules, and one draw needn't show every extreme that they name: `node_ids`: each token names 3 different nodes; the 64 tokens of one device name every node exactly 6 times. Node m holds experts 3 * m to 3 * m + 2. For each j, expert_ids[t, 2 * j] and expert_ids[t, 2 * j + 1] are two different experts of node node_ids[t, j].
All inputs are finite; a program needn't handle non-finite values.
Results may differ from a plain program's by a relative error of at most 0.012.
Values may be sent and summed in bfloat16 or wider, within the bound.
No kernel may reach another device: no remote copies, remote signals or barrier semaphores. Data moves between devices by JAX's collectives and lax.ppermute only.
A program may use at most 192 MiB of HBM per device.

v0:
```python
import jax
import jax.numpy as jnp
from jax import lax
from jax.sharding import PartitionSpec as P


def body(tokens, node_ids, expert_ids, gate_weights, up_weight, down_weight):
    tok_rows, model_width = tokens.shape
    node_count = lax.axis_size("node")
    per_node = up_weight.shape[0]
    capacity = node_ids.shape[1] * tok_rows // node_count
    slot_count = node_count * capacity
    node_grid = jnp.arange(node_count, dtype=jnp.int32)
    picked = jnp.any(node_ids[:, :, None] == node_grid[None, None, :], axis=1).astype(jnp.int32)
    rank_rows = jnp.cumsum(picked, axis=0) - picked
    target = jnp.where(picked > 0, node_grid[None, :] * capacity + rank_rows, -1)
    slot_grid = jnp.arange(slot_count, dtype=jnp.int32)
    placing = (jnp.repeat(target, capacity, axis=1) == slot_grid[None, :]).astype(jnp.bfloat16)
    expert_grid = jnp.arange(node_count * per_node, dtype=jnp.int32)
    flat_gates = jnp.sum(
        jnp.where(
            expert_ids[:, :, None] == expert_grid[None, None, :],
            gate_weights.astype(jnp.float32)[:, :, None],
            0.0,
        ),
        axis=1,
    )
    by_node = jnp.repeat(flat_gates.reshape(tok_rows, node_count, per_node), capacity, axis=1)
    slot_gates = jnp.einsum("ts,tse->se", placing.astype(jnp.float32), by_node)
    outgoing = lax.dot_general(
        placing, tokens, (((0,), (0,)), ((), ())), preferred_element_type=jnp.float32
    ).astype(jnp.bfloat16)
    arrived, arrived_gates = (
        lax.all_to_all(
            outgoing.reshape(node_count, capacity, model_width),
            "node",
            split_axis=0,
            concat_axis=0,
            tiled=True,
        ),
        lax.all_to_all(
            slot_gates.astype(jnp.bfloat16).reshape(node_count, capacity, per_node),
            "node",
            split_axis=0,
            concat_axis=0,
            tiled=True,
        ),
    )
    arrived = arrived.reshape(slot_count, model_width)
    arrived_gates = arrived_gates.reshape(slot_count, per_node)
    pooled, pooled_gates = (
        lax.all_gather(arrived, "local", axis=0, tiled=True),
        lax.all_gather(arrived_gates, "local", axis=0, tiled=True),
    )
    rows_gate = pooled_gates.astype(jnp.float32)
    running = jnp.zeros((slot_count * lax.axis_size("local"), model_width), jnp.float32)
    for expert in range(per_node):
        lifted = jnp.dot(pooled, up_weight[expert], preferred_element_type=jnp.float32)
        scaled = (jax.nn.silu(lifted) * rows_gate[:, expert : expert + 1]).astype(jnp.bfloat16)
        running = running + jnp.dot(scaled, down_weight[expert], preferred_element_type=jnp.float32)
    summed = lax.psum_scatter(
        running.astype(jnp.bfloat16).astype(jnp.float32).astype(jnp.bfloat16),
        "local",
        scatter_dimension=0,
        tiled=True,
    )
    returned = lax.all_to_all(
        summed.reshape(node_count, capacity, model_width),
        "node",
        split_axis=0,
        concat_axis=0,
        tiled=True,
    )
    combined = jnp.dot(
        placing, returned.reshape(slot_count, model_width), preferred_element_type=jnp.float32
    )
    return combined.astype(jnp.bfloat16)


def solution(mesh):
    in_specs = (
        P(("node", "local"), None),
        P(("node", "local"), None),
        P(("node", "local"), None),
        P(("node", "local"), None),
        P("node", None, "local"),
        P("node", "local", None),
    )
    out_specs = P(("node", "local"), None)
    return jax.shard_map(body, mesh=mesh, in_specs=in_specs, out_specs=out_specs, check_vma=False)
```

profile of v0, /device:TPU:1, one launch (start us, length us, event | category | flops | bytes accessed | tf_op | source)
XLA Modules:
  0.0 324.2 jit_solution(444758490590789714)
XLA Ops:
  6.5 0.0 copy-start
  6.5 0.0 all-gather.3.cloned.1.call-start
  6.5 0.8 fusion.40
  7.3 0.1 copy.46
  7.4 0.1 reduce_window_sum.11
  7.5 0.1 copy.47
  7.6 0.0 copy-done
  7.6 1.9 convolution_convert_fusion
  9.6 2.6 reshape.44
  12.2 43.4 %all_to_all.15 = bf16[32,6,5120]{2,1,0:T(8,128)(2,1)} all-to-all(bf16[32,6,5120]{2,1,0:T(8,128)(2,1)S(1)} %reshape.44), channel_id=1, replica_groups=mesh['node'=32,'local'=4] {'node'}, dimensions={0} | all-to-all | bytes 3932160 | tf_op jit(solution)/shard_map/all_to_all | solution.py:34
  55.6 0.0 copy-start.3
  55.6 0.0 copy-start.2
  55.6 4.2 %reshape.45 = bf16[192,5120]{1,0:T(8,128)(2,1)} reshape(bf16[32,6,5120]{2,1,0:T(8,128)(2,1)} %all_to_all.15) | data formatting | bytes 3932160 | tf_op jit(solution)/shard_map/reshape | solution.py:49
  59.8 0.0 all-gather.3.cloned.1.call-update
  59.8 0.0 reduce-scatter.2.cloned.1.call-start
  59.9 0.0 copy-done.3
  59.9 0.0 copy-done.2
  59.9 0.2 select_reduce_fusion
  60.1 0.1 copy.48
  60.2 0.1 broadcast_in_dim.33.clone
  60.3 0.3 fusion.37
  60.7 0.1 copy.57
  60.7 0.1 reshape.48
  60.9 10.7 %all_to_all.16 = bf16[32,6,3]{1,2,0:T(4,128)(2,1)S(1)} all-to-all(bf16[32,6,3]{1,2,0:T(4,128)(2,1)S(1)} %copy.50), channel_id=1, replica_groups=mesh['node'=32,'local'=4] {'node'}, dimensions={0} | all-to-all | bytes 2304 | tf_op jit(solution)/shard_map/all_to_all | solution.py:41
  71.6 0.1 reshape.51
  71.7 10.3 %all-gather = bf16[4,192,3]{1,2,0:T(4,128)(2,1)S(1)} all-gather(bf16[1,192,3]{1,2,0:T(4,128)(2,1)S(1)} %reshape.51), channel_id=1, replica_groups=mesh['node'=32,'local'=4] {'local'}, dimensions={0}, use_global_device_ids=true | all-gather | bytes 5760 | tf_op jit(solution)/shard_map/all_gather | solution.py:53
  82.0 0.1 reshape.53
  82.2 53.9 %all-gather.3.cloned.1.call-done = bf16[768,5120]{1,0:T(8,128)(2,1)} async-done(((bf16[192,5120]{1,0:T(8,128)(2,1)}), bf16[768,5120]{1,0:T(8,128)(2,1)}) %all-gather.3.cloned.1.call-update) | async-done | bytes 7864336 | tf_op jit(solution)/shard_map/all_gather | solution.py:52
  136.1 16.3 %fusion.4 = f32[768,5120]{1,0:T(8,128)} fusion(bf16[3,384,5120]{2,1,0:T(8,128)(2,1)} %param.11, bf16[768,5120]{1,0:T(8,128)(2,1)} %all-gather.3.cloned.1.call-done, bf16[3,5120,384]{2,1,0:T(8,128)(2,1)} %param.10, f32[768]{0:T(1024)S(1)} %get-tuple-element.6), kind=kOutput, calls=%fused_computation.7 | convolution fusion | flops 6041567232 | bytes 31460352 | tf_op jit(solution)/shard_map/dot_general | solution.py:60
  152.3 16.3 %fusion.8 = f32[768,5120]{1,0:T(8,128)} fusion(bf16[3,384,5120]{2,1,0:T(8,128)(2,1)} %param.11, bf16[768,5120]{1,0:T(8,128)(2,1)} %all-gather.3.cloned.1.call-done, bf16[3,5120,384]{2,1,0:T(8,128)(2,1)} %param.10, f32[768]{0:T(1024)S(1)} %get-tuple-element.7), kind=kOutput, calls=%fused_computation.11 | convolution fusion | flops 6041567232 | bytes 31460352 | tf_op jit(solution)/shard_map/dot_general | solution.py:60
  168.6 22.9 %add_convert_fusion = bf16[768,5120]{1,0:T(8,128)(2,1)} fusion(f32[768,5120]{1,0:T(8,128)} %fusion.8, f32[768,5120]{1,0:T(8,128)} %fusion.4, bf16[3,384,5120]{2,1,0:T(8,128)(2,1)} %param.11, bf16[768,5120]{1,0:T(8,128)(2,1)} %all-gather.3.cloned.1.call-done, bf16[3,5120,384]{2,1,0:T(8,128)(2,1)} %param.10, f32[768]{0:T(1024)S(1)} %get-tuple-element.5), kind=kOutput, calls=%fused_computation | convolution fusion | flops 6053363712 | bytes 55053312 | tf_op jit(solution)/shard_map/dot_general | solution.py:60
  191.5 0.0 reduce-scatter.2.cloned.1.call-update
  191.5 77.8 %reduce-scatter.2.cloned.1.call-done = bf16[192,5120]{1,0:T(8,128)(2,1)} async-done(((bf16[768,5120]{1,0:T(8,128)(2,1)}), bf16[192,5120]{1,0:T(8,128)(2,1)}) %reduce-scatter.2.cloned.1.call-update) | async-done | bytes 1966096 | tf_op jit(solution)/shard_map/reduce_scatter | solution.py:61
  269.3 0.0 copy-start.1
  269.4 4.2 %reshape.50 = bf16[32,6,5120]{2,1,0:T(8,128)(2,1)} reshape(bf16[192,5120]{1,0:T(8,128)(2,1)} %reduce-scatter.2.cloned.1.call-done) | data formatting | bytes 3932160 | tf_op jit(solution)/shard_map/reshape | solution.py:68
  273.5 7.7 %all-to-all-start.2 = ((bf16[32,6,5120]{2,1,0:T(8,128)(2,1)}), bf16[32,6,5120]{2,1,0:T(8,128)(2,1)S(1)}, u32[]{:S(2)}, u32[]{:S(2)}) async-start(bf16[32,6,5120]{2,1,0:T(8,128)(2,1)} %reshape.50), calls=%async_computation.3 | async-start | bytes 5242880 | tf_op jit(solution)/shard_map/all_to_all | solution.py:67
  281.3 0.1 broadcast_compare_fusion
  281.4 33.8 %all-to-all-done.2 = bf16[32,6,5120]{2,1,0:T(8,128)(2,1)S(1)} async-done(((bf16[32,6,5120]{2,1,0:T(8,128)(2,1)}), bf16[32,6,5120]{2,1,0:T(8,128)(2,1)S(1)}, u32[]{:S(2)}, u32[]{:S(2)}) %all-to-all-start.2) | async-done | bytes 1966112 | tf_op jit(solution)/shard_map/all_to_all | solution.py:67
  315.2 2.1 fusion
  317.3 0.0 copy-done.1
  (13 shorter events, 0.2 us)
Async XLA Ops:
  6.5 1.1 copy-start
  6.5 129.5 %all-gather.3.cloned.1.call-start = ((), (), s32[]{:S(2)}) async-start(), calls=%async_computation.4 | async-start | bytes 9830400 | tf_op jit(solution)/shard_map/all_gather | solution.py:52
  55.6 4.2 %copy-start.3 = (bf16[64,6]{0,1:T(8,128)(2,1)S(1)}, bf16[64,6]{0,1:T(8,128)(2,1)}, u32[]{:S(2)}) copy-start(bf16[64,6]{0,1:T(8,128)(2,1)} %param.9) | copy-start | bytes 2308
  55.6 4.3 %copy-start.2 = (s32[64,6]{0,1:T(8,128)S(1)}, s32[64,6]{0,1:T(8,128)}, u32[]{:S(2)}) copy-start(s32[64,6]{0,1:T(8,128)} %param.8) | copy-start | bytes 4612
  59.8 209.5 %reduce-scatter.2.cloned.1.call-start = ((), (), s32[]{:S(2)}) async-start(), calls=%async_computation.5 | async-start | bytes 9830400 | tf_op jit(solution)/shard_map/reduce_scatter | solution.py:61
  269.3 48.0 %copy-start.1 = (bf16[64,5120]{1,0:T(8,128)(2,1)S(1)}, bf16[64,5120]{1,0:T(8,128)(2,1)}, u32[]{:S(2)}) copy-start(bf16[64,5120]{1,0:T(8,128)(2,1)} %param.6) | copy-start | bytes 1966084
  273.5 41.7 %all-to-all-start.2 = ((bf16[32,6,5120]{2,1,0:T(8,128)(2,1)}), bf16[32,6,5120]{2,1,0:T(8,128)(2,1)S(1)}, u32[]{:S(2)}, u32[]{:S(2)}) async-start(bf16[32,6,5120]{2,1,0:T(8,128)(2,1)} %reshape.50), calls=%async_computation.3 | async-start | bytes 5242880 | tf_op jit(solution)/shard_map/all_to_all | solution.py:67
Sparse Core Ops, SparseCore 0:
  59.9 76.0 all-gather.2
  191.6 77.6 reduce-scatter.1
where the time goes:
time: 325 us; the launch traced here: 324 us
  waiting for transfers between devices  166 us (51%)
  blocking collectives  64.4 us (20%)
  matrix products  59.9 us (18%)
  between operations  13.6 us (4%)
  local copies, waits for them, and re-layouts  11.9 us (4%)
  starting transfers between devices  7.77 us (2%)
    reduce_scatter x1, waiting for transfers between devices, body(): lax.psum_scatter(running.astype(jnp.bfloat16).astype(jnp.float32).astype(...  77.8 us
    dot_general x3, matrix products, body(): jnp.dot(scaled, down_weight[expert], preferred_element_type=jnp.float32)  55.4 us
    all_gather x1, waiting for transfers between devices, body(): lax.all_gather(arrived, 'local', axis=0, tiled=True)  53.9 us
    all_to_all x1, blocking collectives, body(): lax.all_to_all(outgoing.reshape(node_count, capacity, model_width), 'node...  43.4 us
    all_to_all x1, waiting for transfers between devices, body(): lax.all_to_all(summed.reshape(node_count, capacity, model_width), 'node',...  33.8 us
    all_to_all x1, blocking collectives, body(): lax.all_to_all(slot_gates.astype(jnp.bfloat16).reshape(node_count, capaci...  10.7 us
    all_gather x1, blocking collectives, body(): lax.all_gather(arrived_gates, 'local', axis=0, tiled=True)  10.3 us
    all_to_all x1, starting transfers between devices, body(): lax.all_to_all(summed.reshape(node_count, capacity, model_width), 'node',...  7.73 us
  transfers between devices with their start and end apart: 3, of which 3 were waited for; matrix products, arithmetic and copies ran while one was open for 0% of the time, Pallas kernels for 0%

commit v1 on v0

v1 whole, which is shorter than its diff:
```python
import functools

import jax
import jax.numpy as jnp
from jax import lax
from jax.experimental import pallas as pl
from jax.experimental.pallas import tpu as pltpu
from jax.sharding import PartitionSpec as P


GROUPS = 2
TAIL = 256
STEPS = 4
SMALL = pltpu.CompilerParams(vmem_limit_bytes=16 * 2**20)
LARGE = pltpu.CompilerParams(vmem_limit_bytes=44 * 2**20)
BF = jnp.bfloat16
F32 = jnp.float32


def nt_dot(a, b):
    return lax.dot_general(a, b, (((1,), (1,)), ((), ())), preferred_element_type=F32)


def select_kernel(nodes, group_ranks, per_node, node_ref, expert_ref, gate_ref, tok_ref, *outs):
    place_ref, group_refs = outs[0], outs[1:]
    tok_rows, width = tok_ref.shape
    slots = place_ref.shape[0]
    group_rows = nodes * group_ranks
    ids = node_ref[...]
    grid = lax.broadcasted_iota(jnp.int32, (nodes, tok_rows), 0)
    picked = jnp.zeros((nodes, tok_rows), F32)
    for j in range(ids.shape[0]):
        picked = picked + jnp.where(ids[j : j + 1, :] == grid, 1.0, 0.0)
    before = jnp.where(
        lax.broadcasted_iota(jnp.int32, (tok_rows, tok_rows), 0)
        < lax.broadcasted_iota(jnp.int32, (tok_rows, tok_rows), 1),
        1.0,
        0.0,
    ).astype(BF)
    rank = jnp.dot(picked.astype(BF), before, preferred_element_type=F32)
    rank = jnp.where(picked > 0.5, rank, -1.0).astype(BF)
    slot = lax.broadcasted_iota(jnp.int32, (slots, nodes), 0)
    owner = lax.rem(slot, group_rows) // group_ranks
    spread = jnp.where(
        owner == lax.broadcasted_iota(jnp.int32, (slots, nodes), 1), 1.0, 0.0
    ).astype(BF)
    slot_col = lax.broadcasted_iota(jnp.int32, (slots, 1), 0)
    want = (slot_col // group_rows) * group_ranks + lax.rem(slot_col, group_ranks)
    place = jnp.where(
        jnp.dot(spread, rank, preferred_element_type=F32) == want.astype(F32), 1.0, 0.0
    ).astype(BF)
    place_ref[...] = place
    ids_slot = nt_dot(place, expert_ref[...].astype(F32).astype(BF))
    gates_slot = nt_dot(place, gate_ref[...])
    base = ((lax.rem(slot_col, group_rows) // group_ranks) * per_node).astype(F32)
    lane = lax.broadcasted_iota(jnp.int32, (slots, TAIL), 1)
    tail = jnp.zeros((slots, TAIL), F32)
    for e in range(per_node):
        gate = jnp.sum(jnp.where(ids_slot == base + float(e), gates_slot, 0.0), axis=1, keepdims=True)
        tail = jnp.where(lane == e, gate, tail)
    tail = tail.astype(BF)
    for g, ref in enumerate(group_refs):
        rows = slice(g * group_rows, (g + 1) * group_rows)
        ref[:, width:] = tail[rows]
        ref[:, :width] = jnp.dot(place[rows], tok_ref[...], preferred_element_type=F32).astype(BF)


def select(tokens, node_ids, expert_ids, gate_weights, nodes, per_node):
    tok_rows, width = tokens.shape
    slots = tok_rows * node_ids.shape[1]
    capacity = slots // nodes
    ranks = capacity // GROUPS
    vm = pl.BlockSpec(memory_space=pltpu.VMEM)
    return pl.pallas_call(
        functools.partial(select_kernel, nodes, ranks, per_node),
        out_shape=[jax.ShapeDtypeStruct((slots, tok_rows), BF)]
        + [jax.ShapeDtypeStruct((nodes * ranks, width + TAIL), BF)] * GROUPS,
        in_specs=[vm] * 4,
        out_specs=[vm] * (GROUPS + 1),
        compiler_params=SMALL,
        name="select",
    )(node_ids.T, expert_ids.T, gate_weights.T, tokens)


def up_kernel(own, right, left, far_a, far_b, up, hid, x, acc):
    step = pl.program_id(0)
    width = x.shape[1] - TAIL
    chunk = width // STEPS
    per_node, _, part = up.shape

    @pl.when(step == 0)
    def _():
        at = 0
        for p in (own, right, left, far_a, far_b):
            x[at : at + p.shape[0], :] = p[...]
            at += p.shape[0]

    cols = x[:, pl.ds(pl.multiple_of(step * chunk, 128), chunk)]
    weight = jnp.concatenate([up[e] for e in range(per_node)], axis=1)
    value = jnp.dot(cols, weight, preferred_element_type=F32)

    @pl.when(step == 0)
    def _():
        acc[...] = value

    @pl.when(step > 0)
    def _():
        acc[...] += value

    @pl.when(step == STEPS - 1)
    def _():
        gates = x[:, width:].astype(F32)
        for e in range(per_node):
            piece = slice(e * part, (e + 1) * part)
            v = acc[:, piece]
            hid[:, piece] = (v / (1.0 + jnp.exp(-v)) * gates[:, e : e + 1]).astype(BF)


def cost(rows, width, units):
    return pl.CostEstimate(
        flops=2 * rows * width * units,
        transcendentals=0,
        bytes_accessed=2 * (width * units + rows * width + rows * units),
    )


def up_project(parts, up):
    per_node, width, part = up.shape
    units = per_node * part
    rows = sum(p.shape[0] for p in parts)
    return pl.pallas_call(
        up_kernel,
        grid=(STEPS,),
        out_shape=jax.ShapeDtypeStruct((rows, units), BF),
        in_specs=[pl.BlockSpec(p.shape, lambda i: (0, 0)) for p in parts]
        + [pl.BlockSpec((per_node, width // STEPS, part), lambda i: (0, i, 0))],
        out_specs=pl.BlockSpec((rows, units), lambda i: (0, 0)),
        scratch_shapes=[pltpu.VMEM((rows, width + TAIL), BF), pltpu.VMEM((rows, units), F32)],
        compiler_params=LARGE,
        cost_estimate=cost(rows, width, units),
        name="up",
    )(*parts, up)


def down_kernel(hid, down, *outs):
    per_node, part, chunk = down.shape
    weight = down[...].reshape(per_node * part, chunk)
    value = jnp.dot(hid[...], weight, preferred_element_type=F32).astype(BF)
    at = 0
    for o in outs:
        o[...] = value[at : at + o.shape[0]]
        at += o.shape[0]


def down_project(hid, down, sizes):
    per_node, part, width = down.shape
    rows, units = hid.shape
    chunk = width // STEPS
    return pl.pallas_call(
        down_kernel,
        grid=(STEPS,),
        out_shape=[jax.ShapeDtypeStruct((s, width), BF) for s in sizes],
        in_specs=[
            pl.BlockSpec((rows, units), lambda i: (0, 0)),
            pl.BlockSpec((per_node, part, chunk), lambda i: (0, 0, i)),
        ],
        out_specs=[pl.BlockSpec((s, chunk), lambda i: (0, i)) for s in sizes],
        compiler_params=LARGE,
        cost_estimate=cost(rows, width, units),
        name="down",
    )(hid, down)


def shift(value, by):
    size = lax.axis_size("local")
    return lax.ppermute(value, "local", [(i, (i + by) % size) for i in range(size)])


def to_nodes(value, nodes):
    rows, width = value.shape
    pieces = value.reshape(nodes, rows // nodes, 2, width // 2)
    swapped = lax.all_to_all(pieces, "node", split_axis=0, concat_axis=0, tiled=True)
    return swapped.reshape(rows, width)


def add(*values):
    total = values[0].astype(F32)
    for v in values[1:]:
        total = total + v.astype(F32)
    return total.astype(BF)


def body(tokens, node_ids, expert_ids, gate_weights, up_weight, down_weight):
    nodes = lax.axis_size("node")
    place, *groups = select(
        tokens, node_ids, expert_ids, gate_weights, nodes, up_weight.shape[0]
    )
    half = groups[0].shape[0] // 2
    gathered = []
    for sent in groups:
        own = to_nodes(sent, nodes)
        right, left = shift(own, 1), shift(own, -1)
        far_a, far_b = shift(right[:half], 1), shift(left[half:], -1)
        gathered.append((own, right, left, far_a, far_b))
    returned = []
    for g, parts in enumerate(gathered):
        hid = up_project(parts, up_weight)
        own, right, left, far_a, far_b = down_project(hid, down_weight, [p.shape[0] for p in parts])
        in_a, in_b = shift(far_a, 1), shift(far_b, -1)
        late_left, late_right = left[half:], right[:half]
        if g == len(gathered) - 1:
            late_left, late_right = shift(late_left, 1), shift(late_right, -1)
            soon_left = shift(add(left[:half], in_a), 1)
            soon_right = shift(add(right[half:], in_b), -1)
            total = jnp.concatenate(
                [add(own[:half], soon_left, late_right), add(own[half:], late_left, soon_right)],
                axis=0,
            )
        else:
            left = jnp.concatenate([add(left[:half], in_a), late_left], axis=0)
            right = jnp.concatenate([late_right, add(right[half:], in_b)], axis=0)
            total = add(own, shift(left, 1), shift(right, -1))
        returned.append(to_nodes(total, nodes))
    combined = lax.dot_general(
        place,
        jnp.concatenate(returned, axis=0),
        (((0,), (0,)), ((), ())),
        preferred_element_type=F32,
    )
    return combined.astype(BF)


def solution(mesh):
    in_specs = (
        P(("node", "local"), None),
        P(("node", "local"), None),
        P(("node", "local"), None),
        P(("node", "local"), None),
        P("node", None, "local"),
        P("node", "local", None),
    )
    out_specs = P(("node", "local"), None)

    return jax.shard_map(body, mesh=mesh, in_specs=in_specs, out_specs=out_specs, check_vma=False)
```

time: 325 us -> 239 us (0.74)
  blocking collectives: 64.4 us -> 0 us
  matrix products: 59.9 us -> 1.35 us
  starting transfers between devices: 7.77 us -> 51.2 us
  Pallas kernels: 0 us -> 36.1 us
  waiting for transfers between devices: 166 us -> 134 us
  between operations: 13.6 us -> 0.27 us
  other arithmetic: 1.18 us -> 4.79 us
    reduce_scatter x1 -> x0, waiting for transfers between devices: 77.8 us -> none  [body(): lax.psum_scatter(running.astype(jnp.bfloat16).astype(jnp.float32).astype(...]
    ppermute x0 -> x18, waiting for transfers between devices: none -> 75.5 us  [shift(): lax.ppermute(value, 'local', [(i, (i + by) % size) for i in range(size)])]
    dot_general x6 -> x1, matrix products: 59.9 us -> 1.35 us  [body(): lax.dot_general(place, jnp.concatenate(returned, axis=0), (((0,), (0,)),...]
    all_to_all x2 -> x0, blocking collectives: 54.1 us -> none  [the longest x1 43.4 us: body(): lax.all_to_all(outgoing.reshape(node_count, capacity, model_width), 'node...]
    all_gather x1 -> x0, waiting for transfers between devices: 53.9 us -> none  [body(): lax.all_gather(arrived, 'local', axis=0, tiled=True)]
    pallas_call x0 -> x5, Pallas kernels: none -> 36.1 us  [the longest x2 18.6 us: up_project(): pl.pallas_call(up_kernel, grid=(STEPS,), out_shape=jax.ShapeDtypeStruct((...]
    all_to_all x1 -> x4, waiting for transfers between devices: 33.8 us -> 58.1 us  [to_nodes(): lax.all_to_all(pieces, 'node', split_axis=0, concat_axis=0, tiled=True)]
    ppermute x0 -> x18, starting transfers between devices: none -> 22.6 us  [shift(): lax.ppermute(value, 'local', [(i, (i + by) % size) for i in range(size)])]
  transfers between devices with their start and end apart: 3 -> 22, of which waited for: 3 -> 12; matrix products, arithmetic and copies ran while one was open for 0% -> 5% of each run, Pallas kernels for 0% -> 15%
where the time goes in v1:
time: 239 us; the launch traced here: 238 us
  waiting for transfers between devices  134 us (56%)
  starting transfers between devices  51.2 us (21%)
  Pallas kernels  36.1 us (15%)
  local copies, waits for them, and re-layouts  10.8 us (5%)
  other arithmetic  4.79 us (2%)
    ppermute x18, waiting for transfers between devices, shift(): lax.ppermute(value, 'local', [(i, (i + by) % size) for i in range(size)])  75.5 us
    all_to_all x4, waiting for transfers between devices, to_nodes(): lax.all_to_all(pieces, 'node', split_axis=0, concat_axis=0, tiled=True)  58.1 us
    all_to_all x4, starting transfers between devices, to_nodes(): lax.all_to_all(pieces, 'node', split_axis=0, concat_axis=0, tiled=True)  28.7 us
    ppermute x18, starting transfers between devices, shift(): lax.ppermute(value, 'local', [(i, (i + by) % size) for i in range(size)])  22.6 us
    pallas_call x2, Pallas kernels, up_project(): pl.pallas_call(up_kernel, grid=(STEPS,), out_shape=jax.ShapeDtypeStruct((...  18.6 us
    pallas_call x2, Pallas kernels, down_project(): pl.pallas_call(down_kernel, grid=(STEPS,), out_shape=[jax.ShapeDtypeStruc...  16.6 us
    reshape x4, local copies, waits for them, and re-layouts, to_nodes(): pieces = value.reshape(nodes, rows // nodes, 2, width // 2)  5.78 us
    unnamed x12, local copies, waits for them, and re-layouts  4.79 us
  transfers between devices with their start and end apart: 22, of which 12 were waited for; matrix products, arithmetic and copies ran while one was open for 5% of the time, Pallas kernels for 15%

profile of v1, /device:TPU:1, one launch (start us, length us, event | category | flops | bytes accessed | tf_op | source)
XLA Modules:
  0.0 238.2 jit_solution(5737926604492377077)
XLA Ops:
  0.0 1.1 copy-done
  1.1 0.7 copy-done.1
  1.8 0.7 copy-done.2
  2.5 0.7 copy-done.3
  3.1 0.9 select.1
  4.1 1.2 reshape.24
  5.3 9.4 %all-to-all-start = ((bf16[32,3,2,2688]{3,2,1,0:T(2,128)(2,1)}), bf16[32,3,2,2688]{3,2,1,0:T(2,128)(2,1)S(1)}, u32[]{:S(2)}, u32[]{:S(2)}) async-start(bf16[32,3,2,2688]{3,2,1,0:T(2,128)(2,1)} %reshape.24), calls=%async_computation | async-start | bytes 2064384 | tf_op jit(solution)/shard_map/all_to_all | solution.py:182
  14.7 1.2 reshape.28
  16.0 15.5 %all-to-all-done = bf16[32,3,2,2688]{3,2,1,0:T(2,128)(2,1)S(1)} async-done(((bf16[32,3,2,2688]{3,2,1,0:T(2,128)(2,1)}), bf16[32,3,2,2688]{3,2,1,0:T(2,128)(2,1)S(1)}, u32[]{:S(2)}, u32[]{:S(2)}) %all-to-all-start) | async-done | bytes 1032224 | tf_op jit(solution)/shard_map/all_to_all | solution.py:182
  31.5 4.4 %all-to-all-start.2 = ((bf16[32,3,2,2688]{3,2,1,0:T(2,128)(2,1)}), bf16[32,3,2,2688]{3,2,1,0:T(2,128)(2,1)}, u32[]{:S(2)}, u32[]{:S(2)}) async-start(bf16[32,3,2,2688]{3,2,1,0:T(2,128)(2,1)} %reshape.28), calls=%async_computation.2 | async-start | bytes 2064384 | tf_op jit(solution)/shard_map/all_to_all | solution.py:182
  36.0 1.4 collective-permute-start
  37.4 1.5 collective-permute-start.1
  38.9 13.8 %all-to-all-done.2 = bf16[32,3,2,2688]{3,2,1,0:T(2,128)(2,1)} async-done(((bf16[32,3,2,2688]{3,2,1,0:T(2,128)(2,1)}), bf16[32,3,2,2688]{3,2,1,0:T(2,128)(2,1)}, u32[]{:S(2)}, u32[]{:S(2)}) %all-to-all-start.2) | async-done | bytes 1032224 | tf_op jit(solution)/shard_map/all_to_all | solution.py:182
  52.7 1.3 copy.9
  54.0 1.4 collective-permute-start.8
  55.4 1.5 collective-permute-start.9
  56.9 4.5 %collective-permute-done.right = bf16[96,5376]{1,0:T(8,128)(2,1)S(1)} collective-permute-done((bf16[96,5376]{1,0:T(8,128)(2,1)S(1)}, bf16[96,5376]{1,0:T(8,128)(2,1)S(1)}, u32[]{:S(2)}, u32[]{:S(2)}) %collective-permute-start) | collective-permute-done | bytes 1032224 | tf_op jit(solution)/shard_map/ppermute | solution.py:176
  61.6 2.7 %collective-permute-start.3 = (bf16[48,5376]{1,0:T(8,128)(2,1)S(1)}, bf16[48,5376]{1,0:T(8,128)(2,1)S(1)}, u32[]{:S(2)}, u32[]{:S(2)}) collective-permute-start(bf16[48,5376]{1,0:T(8,128)(2,1)S(1)} %slice.57), channel_id=1, source_target_pairs={{0,3},{1,0},{2,1},{3,2},{4,7},{5,4},{6,5},{7,6},{8,11},{9,8},{10,9... | collective-permute-start | bytes 1548296 | tf_op jit(solution)/shard_map/ppermute | solution.py:176
  64.3 19.2 %collective-permute-done.8.right = bf16[96,5376]{1,0:T(8,128)(2,1)S(1)} collective-permute-done((bf16[96,5376]{1,0:T(8,128)(2,1)S(1)}, bf16[96,5376]{1,0:T(8,128)(2,1)S(1)}, u32[]{:S(2)}, u32[]{:S(2)}) %collective-permute-start.8) | collective-permute-done | bytes 1032224 | tf_op jit(solution)/shard_map/ppermute | solution.py:176
  83.7 2.7 %collective-permute-start.11 = (bf16[48,5376]{1,0:T(8,128)(2,1)S(1)}, bf16[48,5376]{1,0:T(8,128)(2,1)S(1)}, u32[]{:S(2)}, u32[]{:S(2)}) collective-permute-start(bf16[48,5376]{1,0:T(8,128)(2,1)S(1)} %slice.59), channel_id=1, source_target_pairs={{0,3},{1,0},{2,1},{3,2},{4,7},{5,4},{6,5},{7,6},{8,11},{9,8},{10,9... | collective-permute-start | bytes 1548296 | tf_op jit(solution)/shard_map/ppermute | solution.py:176
  86.5 8.2 %collective-permute-done.2.far_a = bf16[48,5376]{1,0:T(8,128)(2,1)S(1)} collective-permute-done((bf16[48,5376]{1,0:T(8,128)(2,1)S(1)}, bf16[48,5376]{1,0:T(8,128)(2,1)S(1)}, u32[]{:S(2)}, u32[]{:S(2)}) %collective-permute-start.2) | collective-permute-done | bytes 516128 | tf_op jit(solution)/shard_map/ppermute | solution.py:176
  94.6 9.3 %up.4.hid = bf16[384,1152]{1,0:T(8,128)(2,1)S(1)} custom-call(bf16[96,5376]{1,0:T(8,128)(2,1)S(1)} %bitcast.21, bf16[96,5376]{1,0:T(8,128)(2,1)S(1)} %collective-permute-done.right, bf16[96,5376]{1,0:T(8,128)(2,1)S(1)} %collective-permute-done.1.left, bf16[48,5376]{1,0:T(8,128)(2,1)S(1)} %collective-permute-done.2.far_a, ...), custom_call_target="tpu_custom_call" | custom-call | flops 4529848320 | bytes 16613376 | tf_op jit(solution)/shard_map/up/pallas_call | solution.py:131
  103.9 8.3 %down.4 = (bf16[96,5120]{1,0:T(8,128)(2,1)S(1)}, bf16[96,5120]{1,0:T(8,128)(2,1)S(1)}, bf16[96,5120]{1,0:T(8,128)(2,1)S(1)}, bf16[48,5120]{1,0:T(8,128)(2,1)S(1)}, bf16[48,5120]{1,0:T(8,128)(2,1)S(1)}) custom-call(bf16[384,1152]{1,0:T(8,128)(2,1)S(1)} %up.4.hid, bf16[3,384,5120]{2,1,0:T(8,128)(2,1)} %down.7), custom_call_target="tpu_custom_call" | custom-call | flops 4529848320 | bytes 16613376 | tf_op jit(solution)/shard_map/down/pallas_call | solution.py:159
  112.2 1.0 collective-permute-start.4
  113.3 2.0 collective-permute-start.6
  115.2 9.3 %up.6.hid = bf16[384,1152]{1,0:T(8,128)(2,1)S(1)} custom-call(bf16[96,5376]{1,0:T(8,128)(2,1)S(1)} %bitcast.18, bf16[96,5376]{1,0:T(8,128)(2,1)S(1)} %collective-permute-done.8.right, bf16[96,5376]{1,0:T(8,128)(2,1)S(1)} %collective-permute-done.9.left, bf16[48,5376]{1,0:T(8,128)(2,1)S(1)} %collective-permute-done.10.far_a, ...), custom_call_target="tpu_custom_call" | custom-call | flops 4529848320 | bytes 16613376 | tf_op jit(solution)/shard_map/up/pallas_call | solution.py:131
  124.6 8.3 %down.6 = (bf16[96,5120]{1,0:T(8,128)(2,1)S(1)}, bf16[96,5120]{1,0:T(8,128)(2,1)S(1)}, bf16[96,5120]{1,0:T(8,128)(2,1)S(1)}, bf16[48,5120]{1,0:T(8,128)(2,1)S(1)}, bf16[48,5120]{1,0:T(8,128)(2,1)S(1)}) custom-call(bf16[384,1152]{1,0:T(8,128)(2,1)S(1)} %up.6.hid, bf16[3,384,5120]{2,1,0:T(8,128)(2,1)} %down.7), custom_call_target="tpu_custom_call" | custom-call | flops 4529848320 | bytes 16613376 | tf_op jit(solution)/shard_map/down/pallas_call | solution.py:159
  132.9 1.4 collective-permute-start.16
  134.4 2.6 %collective-permute-start.14 = (bf16[48,5120]{1,0:T(8,128)(2,1)S(1)}, bf16[48,5120]{1,0:T(8,128)(2,1)S(1)}, u32[]{:S(2)}, u32[]{:S(2)}) collective-permute-start(bf16[48,5120]{1,0:T(8,128)(2,1)S(1)} %slice.52), channel_id=1, source_target_pairs={{0,3},{1,0},{2,1},{3,2},{4,7},{5,4},{6,5},{7,6},{8,11},{9,8},{10,9... | collective-permute-start | bytes 1474568 | tf_op jit(solution)/shard_map/ppermute | solution.py:176
  137.3 1.0 pad_maximum_fusion
  138.3 4.6 %collective-permute-done.16 = bf16[48,5120]{1,0:T(8,128)(2,1)S(1)} collective-permute-done((bf16[48,5120]{1,0:T(8,128)(2,1)S(1)}, bf16[48,5120]{1,0:T(8,128)(2,1)S(1)}, u32[]{:S(2)}, u32[]{:S(2)}) %collective-permute-start.16) | collective-permute-done | bytes 491552 | tf_op jit(solution)/shard_map/ppermute | solution.py:176
  143.1 2.1 collective-permute-done.12
  145.2 0.7 collective-permute-start.17
  146.0 0.9 collective-permute-start.13
  146.9 1.0 pad_maximum_fusion.1
  148.0 5.5 %collective-permute-done.14 = bf16[48,5120]{1,0:T(8,128)(2,1)S(1)} collective-permute-done((bf16[48,5120]{1,0:T(8,128)(2,1)S(1)}, bf16[48,5120]{1,0:T(8,128)(2,1)S(1)}, u32[]{:S(2)}, u32[]{:S(2)}) %collective-permute-start.14) | collective-permute-done | bytes 491552 | tf_op jit(solution)/shard_map/ppermute | solution.py:176
  153.5 2.5 %collective-permute-start.7 = (bf16[96,5120]{1,0:T(8,128)(2,1)}, bf16[96,5120]{1,0:T(8,128)(2,1)}, u32[]{:S(2)}, u32[]{:S(2)}) collective-permute-start(bf16[96,5120]{1,0:T(8,128)(2,1)} %pad_maximum_fusion.1), channel_id=1, source_target_pairs={{0,3},{1,0},{2,1},{3,2},{4,7},{5,4},{6,5},{7,6},{8,11},{9,8},{10,9... | collective-permute-start | bytes 2949128 | tf_op jit(solution)/shard_map/ppermute | solution.py:176
  156.0 8.2 %collective-permute-done.17 = bf16[48,5120]{1,0:T(8,128)(2,1)S(1)} collective-permute-done((bf16[48,5120]{1,0:T(8,128)(2,1)S(1)}, bf16[48,5120]{1,0:T(8,128)(2,1)S(1)}, u32[]{:S(2)}, u32[]{:S(2)}) %collective-permute-start.17) | collective-permute-done | bytes 491552 | tf_op jit(solution)/shard_map/ppermute | solution.py:176
  164.1 23.2 %collective-permute-done.13 = bf16[48,5120]{1,0:T(8,128)(2,1)S(1)} collective-permute-done((bf16[48,5120]{1,0:T(8,128)(2,1)S(1)}, bf16[48,5120]{1,0:T(8,128)(2,1)S(1)}, u32[]{:S(2)}, u32[]{:S(2)}) %collective-permute-start.13) | collective-permute-done | bytes 491552 | tf_op jit(solution)/shard_map/ppermute | solution.py:176
  187.3 0.4 add_convert_fusion.3
  187.7 1.7 reshape.30
  189.4 10.9 %all-to-all-start.3 = ((bf16[32,3,2,2560]{3,2,1,0:T(2,128)(2,1)}), bf16[32,3,2,2560]{3,2,1,0:T(2,128)(2,1)S(1)}, u32[]{:S(2)}, u32[]{:S(2)}) async-start(bf16[32,3,2,2560]{3,2,1,0:T(2,128)(2,1)} %reshape.30), calls=%async_computation.3 | async-start | bytes 1966080 | tf_op jit(solution)/shard_map/all_to_all | solution.py:182
  200.3 1.9 add_convert_fusion
  202.2 1.7 reshape.26
  203.8 12.7 %all-to-all-done.3 = bf16[32,3,2,2560]{3,2,1,0:T(2,128)(2,1)S(1)} async-done(((bf16[32,3,2,2560]{3,2,1,0:T(2,128)(2,1)}), bf16[32,3,2,2560]{3,2,1,0:T(2,128)(2,1)S(1)}, u32[]{:S(2)}, u32[]{:S(2)}) %all-to-all-start.3) | async-done | bytes 983072 | tf_op jit(solution)/shard_map/all_to_all | solution.py:182
  216.5 3.9 %all-to-all-start.1 = ((bf16[32,3,2,2560]{3,2,1,0:T(2,128)(2,1)}), bf16[32,3,2,2560]{3,2,1,0:T(2,128)(2,1)S(1)}, u32[]{:S(2)}, u32[]{:S(2)}) async-start(bf16[32,3,2,2560]{3,2,1,0:T(2,128)(2,1)} %reshape.26), calls=%async_computation.1 | async-start | bytes 1966080 | tf_op jit(solution)/shard_map/all_to_all | solution.py:182
  220.6 16.1 %all-to-all-done.1 = bf16[32,3,2,2560]{3,2,1,0:T(2,128)(2,1)S(1)} async-done(((bf16[32,3,2,2560]{3,2,1,0:T(2,128)(2,1)}), bf16[32,3,2,2560]{3,2,1,0:T(2,128)(2,1)S(1)}, u32[]{:S(2)}, u32[]{:S(2)}) %all-to-all-start.1) | async-done | bytes 983072 | tf_op jit(solution)/shard_map/all_to_all | solution.py:182
  236.8 1.4 convolution_convert_fusion
  (35 shorter events, 1.5 us)
Async XLA Ops:
  0.0 1.1 copy-start
  1.1 0.7 copy-start.1
  1.8 0.7 copy-start.2
  2.5 0.7 copy-start.3
  5.3 26.2 %all-to-all-start = ((bf16[32,3,2,2688]{3,2,1,0:T(2,128)(2,1)}), bf16[32,3,2,2688]{3,2,1,0:T(2,128)(2,1)S(1)}, u32[]{:S(2)}, u32[]{:S(2)}) async-start(bf16[32,3,2,2688]{3,2,1,0:T(2,128)(2,1)} %reshape.24), calls=%async_computation | async-start | bytes 2064384 | tf_op jit(solution)/shard_map/all_to_all | solution.py:182
  31.5 21.2 %all-to-all-start.2 = ((bf16[32,3,2,2688]{3,2,1,0:T(2,128)(2,1)}), bf16[32,3,2,2688]{3,2,1,0:T(2,128)(2,1)}, u32[]{:S(2)}, u32[]{:S(2)}) async-start(bf16[32,3,2,2688]{3,2,1,0:T(2,128)(2,1)} %reshape.28), calls=%async_computation.2 | async-start | bytes 2064384 | tf_op jit(solution)/shard_map/all_to_all | solution.py:182
  36.0 25.4 %collective-permute-start = (bf16[96,5376]{1,0:T(8,128)(2,1)S(1)}, bf16[96,5376]{1,0:T(8,128)(2,1)S(1)}, u32[]{:S(2)}, u32[]{:S(2)}) collective-permute-start(bf16[96,5376]{1,0:T(8,128)(2,1)S(1)} %bitcast.19), channel_id=1, source_target_pairs={{0,1},{1,2},{2,3},{3,0},{4,5},{5,6},{6,7},{7,4},{8,9},{9,10},{10,1... | collective-permute-start | bytes 3096584 | tf_op jit(solution)/shard_map/ppermute | solution.py:176
  37.4 24.2 %collective-permute-start.1 = (bf16[96,5376]{1,0:T(8,128)(2,1)S(1)}, bf16[96,5376]{1,0:T(8,128)(2,1)S(1)}, u32[]{:S(2)}, u32[]{:S(2)}) collective-permute-start(bf16[96,5376]{1,0:T(8,128)(2,1)S(1)} %bitcast.20), channel_id=1, source_target_pairs={{0,3},{1,0},{2,1},{3,2},{4,7},{5,4},{6,5},{7,6},{8,11},{9,8},{10,9... | collective-permute-start | bytes 3096584 | tf_op jit(solution)/shard_map/ppermute | solution.py:176
  54.0 29.5 %collective-permute-start.8 = (bf16[96,5376]{1,0:T(8,128)(2,1)S(1)}, bf16[96,5376]{1,0:T(8,128)(2,1)S(1)}, u32[]{:S(2)}, u32[]{:S(2)}) collective-permute-start(bf16[96,5376]{1,0:T(8,128)(2,1)S(1)} %bitcast.16), channel_id=1, source_target_pairs={{0,1},{1,2},{2,3},{3,0},{4,5},{5,6},{6,7},{7,4},{8,9},{9,10},{10,1... | collective-permute-start | bytes 3096584 | tf_op jit(solution)/shard_map/ppermute | solution.py:176
  55.4 28.3 %collective-permute-start.9 = (bf16[96,5376]{1,0:T(8,128)(2,1)S(1)}, bf16[96,5376]{1,0:T(8,128)(2,1)S(1)}, u32[]{:S(2)}, u32[]{:S(2)}) collective-permute-start(bf16[96,5376]{1,0:T(8,128)(2,1)S(1)} %bitcast.17), channel_id=1, source_target_pairs={{0,3},{1,0},{2,1},{3,2},{4,7},{5,4},{6,5},{7,6},{8,11},{9,8},{10,9... | collective-permute-start | bytes 3096584 | tf_op jit(solution)/shard_map/ppermute | solution.py:176
  61.5 33.1 %collective-permute-start.2 = (bf16[48,5376]{1,0:T(8,128)(2,1)S(1)}, bf16[48,5376]{1,0:T(8,128)(2,1)S(1)}, u32[]{:S(2)}, u32[]{:S(2)}) collective-permute-start(bf16[48,5376]{1,0:T(8,128)(2,1)S(1)} %slice.56), channel_id=1, source_target_pairs={{0,1},{1,2},{2,3},{3,0},{4,5},{5,6},{6,7},{7,4},{8,9},{9,10},{10,1... | collective-permute-start | bytes 1548296 | tf_op jit(solution)/shard_map/ppermute | solution.py:176
  61.6 33.0 %collective-permute-start.3 = (bf16[48,5376]{1,0:T(8,128)(2,1)S(1)}, bf16[48,5376]{1,0:T(8,128)(2,1)S(1)}, u32[]{:S(2)}, u32[]{:S(2)}) collective-permute-start(bf16[48,5376]{1,0:T(8,128)(2,1)S(1)} %slice.57), channel_id=1, source_target_pairs={{0,3},{1,0},{2,1},{3,2},{4,7},{5,4},{6,5},{7,6},{8,11},{9,8},{10,9... | collective-permute-start | bytes 1548296 | tf_op jit(solution)/shard_map/ppermute | solution.py:176
  83.6 31.6 %collective-permute-start.10 = (bf16[48,5376]{1,0:T(8,128)(2,1)S(1)}, bf16[48,5376]{1,0:T(8,128)(2,1)S(1)}, u32[]{:S(2)}, u32[]{:S(2)}) collective-permute-start(bf16[48,5376]{1,0:T(8,128)(2,1)S(1)} %slice.58), channel_id=1, source_target_pairs={{0,1},{1,2},{2,3},{3,0},{4,5},{5,6},{6,7},{7,4},{8,9},{9,10},{10,1... | collective-permute-start | bytes 1548296 | tf_op jit(solution)/shard_map/ppermute | solution.py:176
  83.7 31.5 %collective-permute-start.11 = (bf16[48,5376]{1,0:T(8,128)(2,1)S(1)}, bf16[48,5376]{1,0:T(8,128)(2,1)S(1)}, u32[]{:S(2)}, u32[]{:S(2)}) collective-permute-start(bf16[48,5376]{1,0:T(8,128)(2,1)S(1)} %slice.59), channel_id=1, source_target_pairs={{0,3},{1,0},{2,1},{3,2},{4,7},{5,4},{6,5},{7,6},{8,11},{9,8},{10,9... | collective-permute-start | bytes 1548296 | tf_op jit(solution)/shard_map/ppermute | solution.py:176
  112.2 24.9 %collective-permute-start.4 = (bf16[48,5120]{1,0:T(8,128)(2,1)S(1)}, bf16[48,5120]{1,0:T(8,128)(2,1)S(1)}, u32[]{:S(2)}, u32[]{:S(2)}) collective-permute-start(bf16[48,5120]{1,0:T(8,128)(2,1)S(1)} %get-tuple-element.22), channel_id=1, source_target_pairs={{0,1},{1,2},{2,3},{3,0},{4,5},{5,6},{6,7},{7,4},{8,9},{9,10},{10,1... | collective-permute-start | bytes 1474568 | tf_op jit(solution)/shard_map/ppermute | solution.py:176
  113.3 32.7 %collective-permute-start.6 = (bf16[48,5120]{1,0:T(8,128)(2,1)S(1)}, bf16[48,5120]{1,0:T(8,128)(2,1)S(1)}, u32[]{:S(2)}, u32[]{:S(2)}) collective-permute-start(bf16[48,5120]{1,0:T(8,128)(2,1)S(1)} %get-tuple-element.24), channel_id=1, source_target_pairs={{0,3},{1,0},{2,1},{3,2},{4,7},{5,4},{6,5},{7,6},{8,11},{9,8},{10,9... | collective-permute-start | bytes 1474568 | tf_op jit(solution)/shard_map/ppermute | solution.py:176
  132.9 10.1 %collective-permute-start.16 = (bf16[48,5120]{1,0:T(8,128)(2,1)S(1)}, bf16[48,5120]{1,0:T(8,128)(2,1)S(1)}, u32[]{:S(2)}, u32[]{:S(2)}) collective-permute-start(bf16[48,5120]{1,0:T(8,128)(2,1)S(1)} %get-tuple-element.30), channel_id=1, source_target_pairs={{0,3},{1,0},{2,1},{3,2},{4,7},{5,4},{6,5},{7,6},{8,11},{9,8},{10,9... | collective-permute-start | bytes 1474568 | tf_op jit(solution)/shard_map/ppermute | solution.py:176
  134.3 10.9 %collective-permute-start.12 = (bf16[48,5120]{1,0:T(8,128)(2,1)S(1)}, bf16[48,5120]{1,0:T(8,128)(2,1)S(1)}, u32[]{:S(2)}, u32[]{:S(2)}) collective-permute-start(bf16[48,5120]{1,0:T(8,128)(2,1)S(1)} %get-tuple-element.28), channel_id=1, source_target_pairs={{0,1},{1,2},{2,3},{3,0},{4,5},{5,6},{6,7},{7,4},{8,9},{9,10},{10,1... | collective-permute-start | bytes 1474568 | tf_op jit(solution)/shard_map/ppermute | solution.py:176
  134.4 19.1 %collective-permute-start.14 = (bf16[48,5120]{1,0:T(8,128)(2,1)S(1)}, bf16[48,5120]{1,0:T(8,128)(2,1)S(1)}, u32[]{:S(2)}, u32[]{:S(2)}) collective-permute-start(bf16[48,5120]{1,0:T(8,128)(2,1)S(1)} %slice.52), channel_id=1, source_target_pairs={{0,3},{1,0},{2,1},{3,2},{4,7},{5,4},{6,5},{7,6},{8,11},{9,8},{10,9... | collective-permute-start | bytes 1474568 | tf_op jit(solution)/shard_map/ppermute | solution.py:176
  137.1 18.9 %collective-permute-start.15 = (bf16[48,5120]{1,0:T(8,128)(2,1)S(1)}, bf16[48,5120]{1,0:T(8,128)(2,1)S(1)}, u32[]{:S(2)}, u32[]{:S(2)}) collective-permute-start(bf16[48,5120]{1,0:T(8,128)(2,1)S(1)} %slice.54), channel_id=1, source_target_pairs={{0,1},{1,2},{2,3},{3,0},{4,5},{5,6},{6,7},{7,4},{8,9},{9,10},{10,1... | collective-permute-start | bytes 1474568 | tf_op jit(solution)/shard_map/ppermute | solution.py:176
  143.0 57.3 %collective-permute-start.5 = (bf16[96,5120]{1,0:T(8,128)(2,1)}, bf16[96,5120]{1,0:T(8,128)(2,1)}, u32[]{:S(2)}, u32[]{:S(2)}) collective-permute-start(bf16[96,5120]{1,0:T(8,128)(2,1)} %pad_maximum_fusion), channel_id=1, source_target_pairs={{0,1},{1,2},{2,3},{3,0},{4,5},{5,6},{6,7},{7,4},{8,9},{9,10},{10,1... | collective-permute-start | bytes 2949128 | tf_op jit(solution)/shard_map/ppermute | solution.py:176
  145.2 19.0 %collective-permute-start.17 = (bf16[48,5120]{1,0:T(8,128)(2,1)S(1)}, bf16[48,5120]{1,0:T(8,128)(2,1)S(1)}, u32[]{:S(2)}, u32[]{:S(2)}) collective-permute-start(bf16[48,5120]{1,0:T(8,128)(2,1)S(1)} %add_convert_fusion.2), channel_id=1, source_target_pairs={{0,3},{1,0},{2,1},{3,2},{4,7},{5,4},{6,5},{7,6},{8,11},{9,8},{10,9... | collective-permute-start | bytes 1474568 | tf_op jit(solution)/shard_map/ppermute | solution.py:176
  146.0 41.3 %collective-permute-start.13 = (bf16[48,5120]{1,0:T(8,128)(2,1)S(1)}, bf16[48,5120]{1,0:T(8,128)(2,1)S(1)}, u32[]{:S(2)}, u32[]{:S(2)}) collective-permute-start(bf16[48,5120]{1,0:T(8,128)(2,1)S(1)} %add_convert_fusion.4), channel_id=1, source_target_pairs={{0,1},{1,2},{2,3},{3,0},{4,5},{5,6},{6,7},{7,4},{8,9},{9,10},{10,1... | collective-permute-start | bytes 1474568 | tf_op jit(solution)/shard_map/ppermute | solution.py:176
  153.5 46.8 %collective-permute-start.7 = (bf16[96,5120]{1,0:T(8,128)(2,1)}, bf16[96,5120]{1,0:T(8,128)(2,1)}, u32[]{:S(2)}, u32[]{:S(2)}) collective-permute-start(bf16[96,5120]{1,0:T(8,128)(2,1)} %pad_maximum_fusion.1), channel_id=1, source_target_pairs={{0,3},{1,0},{2,1},{3,2},{4,7},{5,4},{6,5},{7,6},{8,11},{9,8},{10,9... | collective-permute-start | bytes 2949128 | tf_op jit(solution)/shard_map/ppermute | solution.py:176
  189.4 27.1 %all-to-all-start.3 = ((bf16[32,3,2,2560]{3,2,1,0:T(2,128)(2,1)}), bf16[32,3,2,2560]{3,2,1,0:T(2,128)(2,1)S(1)}, u32[]{:S(2)}, u32[]{:S(2)}) async-start(bf16[32,3,2,2560]{3,2,1,0:T(2,128)(2,1)} %reshape.30), calls=%async_computation.3 | async-start | bytes 1966080 | tf_op jit(solution)/shard_map/all_to_all | solution.py:182
  216.5 20.1 %all-to-all-start.1 = ((bf16[32,3,2,2560]{3,2,1,0:T(2,128)(2,1)}), bf16[32,3,2,2560]{3,2,1,0:T(2,128)(2,1)S(1)}, u32[]{:S(2)}, u32[]{:S(2)}) async-start(bf16[32,3,2,2560]{3,2,1,0:T(2,128)(2,1)} %reshape.26), calls=%async_computation.1 | async-start | bytes 1966080 | tf_op jit(solution)/shard_map/all_to_all | solution.py:182

commit v2 on v1

--- a/solution.py
+++ b/solution.py
@@ -10,6 +10,7 @@
 
 GROUPS = 2
 TAIL = 256
+LANES = 128
 STEPS = 4
 SMALL = pltpu.CompilerParams(vmem_limit_bytes=16 * 2**20)
 LARGE = pltpu.CompilerParams(vmem_limit_bytes=44 * 2**20)
@@ -21,7 +22,16 @@
     return lax.dot_general(a, b, (((1,), (1,)), ((), ())), preferred_element_type=F32)
 
 
-def select_kernel(nodes, group_ranks, per_node, node_ref, expert_ref, gate_ref, tok_ref, *outs):
+def select_kernel(nodes, group_ranks, per_node, *refs):
+    sources, outs, copies, sems = refs[:4], refs[4 : 5 + GROUPS], refs[5 + GROUPS : -1], refs[-1]
+    moves = [
+        pltpu.make_async_copy(s, c, sems.at[i]) for i, (s, c) in enumerate(zip(sources, copies))
+    ]
+    for m in moves:
+        m.start()
+    for m in moves:
+        m.wait()
+    node_ref, expert_ref, gate_ref, tok_ref = copies
     place_ref, group_refs = outs[0], outs[1:]
     tok_rows, width = tok_ref.shape
     slots = place_ref.shape[0]
@@ -53,15 +63,16 @@
     ids_slot = nt_dot(place, expert_ref[...].astype(F32).astype(BF))
     gates_slot = nt_dot(place, gate_ref[...])
     base = ((lax.rem(slot_col, group_rows) // group_ranks) * per_node).astype(F32)
-    lane = lax.broadcasted_iota(jnp.int32, (slots, TAIL), 1)
-    tail = jnp.zeros((slots, TAIL), F32)
+    lane = lax.broadcasted_iota(jnp.int32, (group_rows, TAIL), 1)
+    tail = jnp.zeros((group_rows, TAIL), F32)
     for e in range(per_node):
         gate = jnp.sum(jnp.where(ids_slot == base + float(e), gates_slot, 0.0), axis=1, keepdims=True)
-        tail = jnp.where(lane == e, gate, tail)
-    tail = tail.astype(BF)
+        for g in range(GROUPS):
+            rows = slice(g * group_rows, (g + 1) * group_rows)
+            tail = jnp.where(lane == g * per_node + e, gate[rows], tail)
+    group_refs[0][:, width:] = tail.astype(BF)
     for g, ref in enumerate(group_refs):
         rows = slice(g * group_rows, (g + 1) * group_rows)
-        ref[:, width:] = tail[rows]
         ref[:, :width] = jnp.dot(place[rows], tok_ref[...], preferred_element_type=F32).astype(BF)
 
 
@@ -71,28 +82,35 @@
     capacity = slots // nodes
     ranks = capacity // GROUPS
     vm = pl.BlockSpec(memory_space=pltpu.VMEM)
+    operands = (node_ids.T, expert_ids.T, gate_weights.T, tokens)
     return pl.pallas_call(
         functools.partial(select_kernel, nodes, ranks, per_node),
         out_shape=[jax.ShapeDtypeStruct((slots, tok_rows), BF)]
-        + [jax.ShapeDtypeStruct((nodes * ranks, width + TAIL), BF)] * GROUPS,
-        in_specs=[vm] * 4,
+        + [
+            jax.ShapeDtypeStruct((nodes * ranks, width + (TAIL if g == 0 else 0)), BF)
+            for g in range(GROUPS)
+        ],
+        in_specs=[pl.BlockSpec(memory_space=pltpu.HBM)] * 4,
         out_specs=[vm] * (GROUPS + 1),
+        scratch_shapes=[pltpu.VMEM(v.shape, v.dtype) for v in operands]
+        + [pltpu.SemaphoreType.DMA((len(operands),))],
         compiler_params=SMALL,
         name="select",
-    )(node_ids.T, expert_ids.T, gate_weights.T, tokens)
-
-
-def up_kernel(own, right, left, far_a, far_b, up, hid, x, acc):
+    )(*operands)
+
+
+def up_kernel(parts, gate_parts, first_gate, *refs):
+    xs, gate_refs = refs[:parts], refs[parts : parts + gate_parts]
+    up, hid, x, acc = refs[parts + gate_parts :]
     step = pl.program_id(0)
-    width = x.shape[1] - TAIL
-    chunk = width // STEPS
+    chunk = x.shape[1] // STEPS
     per_node, _, part = up.shape
 
     @pl.when(step == 0)
     def _():
         at = 0
-        for p in (own, right, left, far_a, far_b):
-            x[at : at + p.shape[0], :] = p[...]
+        for p in xs:
+            x[at : at + p.shape[0], :] = p[:, : x.shape[1]]
             at += p.shape[0]
 
     cols = x[:, pl.ds(pl.multiple_of(step * chunk, 128), chunk)]
@@ -109,11 +127,11 @@
 
     @pl.when(step == STEPS - 1)
     def _():
-        gates = x[:, width:].astype(F32)
+        gates = jnp.concatenate([r[...] for r in gate_refs], axis=0).astype(F32)
         for e in range(per_node):
             piece = slice(e * part, (e + 1) * part)
             v = acc[:, piece]
-            hid[:, piece] = (v / (1.0 + jnp.exp(-v)) * gates[:, e : e + 1]).astype(BF)
+            hid[:, piece] = (v / (1.0 + jnp.exp(-v)) * gates[:, first_gate + e : first_gate + e + 1]).astype(BF)
 
 
 def cost(rows, width, units):
@@ -124,22 +142,23 @@
     )
 
 
-def up_project(parts, up):
+def up_project(parts, gate_parts, first_gate, up):
     per_node, width, part = up.shape
     units = per_node * part
     rows = sum(p.shape[0] for p in parts)
     return pl.pallas_call(
-        up_kernel,
+        functools.partial(up_kernel, len(parts), len(gate_parts), first_gate),
         grid=(STEPS,),
         out_shape=jax.ShapeDtypeStruct((rows, units), BF),
         in_specs=[pl.BlockSpec(p.shape, lambda i: (0, 0)) for p in parts]
+        + [pl.BlockSpec((p.shape[0], LANES), lambda i: (0, width // LANES)) for p in gate_parts]
         + [pl.BlockSpec((per_node, width // STEPS, part), lambda i: (0, i, 0))],
         out_specs=pl.BlockSpec((rows, units), lambda i: (0, 0)),
-        scratch_shapes=[pltpu.VMEM((rows, width + TAIL), BF), pltpu.VMEM((rows, units), F32)],
+        scratch_shapes=[pltpu.VMEM((rows, width), BF), pltpu.VMEM((rows, units), F32)],
         compiler_params=LARGE,
         cost_estimate=cost(rows, width, units),
         name="up",
-    )(*parts, up)
+    )(*parts, *gate_parts, up)
 
 
 def down_kernel(hid, down, *outs):
@@ -197,15 +216,23 @@
     )
     half = groups[0].shape[0] // 2
     gathered = []
-    for sent in groups:
+    for g, sent in enumerate(groups):
         own = to_nodes(sent, nodes)
-        right, left = shift(own, 1), shift(own, -1)
-        far_a, far_b = shift(right[:half], 1), shift(left[half:], -1)
-        gathered.append((own, right, left, far_a, far_b))
+        if g == 0:
+            top, low = own[:half], own[half:]
+            right_top, left_low = shift(top, 1), shift(low, -1)
+            right_low, left_top = shift(low, 1), shift(top, -1)
+            far_a, far_b = shift(right_top, 1), shift(left_low, -1)
+            parts = (top, low, right_top, right_low, left_top, left_low, far_a, far_b)
+        else:
+            right, left = shift(own, 1), shift(own, -1)
+            far_a, far_b = shift(right[:half], 1), shift(left[half:], -1)
+            parts = (own, right, left, far_a, far_b)
+        gathered.append(parts)
     returned = []
     for g, parts in enumerate(gathered):
-        hid = up_project(parts, up_weight)
-        own, right, left, far_a, far_b = down_project(hid, down_weight, [p.shape[0] for p in parts])
+        hid = up_project(parts, gathered[0], g * up_weight.shape[0], up_weight)
+        own, right, left, far_a, far_b = down_project(hid, down_weight, [2 * half] * 3 + [half] * 2)
         in_a, in_b = shift(far_a, 1), shift(far_b, -1)
         late_left, late_right = left[half:], right[:half]
         if g == len(gathered) - 1:

time: 239 us -> 251 us (1.050)
  waiting for transfers between devices: 134 us -> 149 us
  starting transfers between devices: 51.2 us -> 47.4 us
    ppermute x18 -> x20, waiting for transfers between devices: 75.5 us -> 91.5 us  [shift(): lax.ppermute(value, 'local', [(i, (i + by) % size) for i in range(size)])]
    all_to_all x4, starting transfers between devices: 28.7 us -> 24 us  [to_nodes(): lax.all_to_all(pieces, 'node', split_axis=0, concat_axis=0, tiled=True)]
    ppermute x18 -> x20, starting transfers between devices: 22.6 us -> 23.3 us  [shift(): lax.ppermute(value, 'local', [(i, (i + by) % size) for i in range(size)])]
  transfers between devices with their start and end apart: 22 -> 24, of which waited for: 12 -> 12; matrix products, arithmetic and copies ran while one was open for 5% -> 4% of each run, Pallas kernels for 15% -> 14%
where the time goes in v2:
time: 251 us; the launch traced here: 250 us
  waiting for transfers between devices  149 us (59%)
  starting transfers between devices  47.4 us (19%)
  Pallas kernels  36.5 us (15%)
  local copies, waits for them, and re-layouts  11.9 us (5%)
  other arithmetic  3.82 us (2%)
    ppermute x20, waiting for transfers between devices, shift(): lax.ppermute(value, 'local', [(i, (i + by) % size) for i in range(size)])  91.5 us
    all_to_all x4, waiting for transfers between devices, to_nodes(): lax.all_to_all(pieces, 'node', split_axis=0, concat_axis=0, tiled=True)  57.7 us
    all_to_all x4, starting transfers between devices, to_nodes(): lax.all_to_all(pieces, 'node', split_axis=0, concat_axis=0, tiled=True)  24 us
    ppermute x20, starting transfers between devices, shift(): lax.ppermute(value, 'local', [(i, (i + by) % size) for i in range(size)])  23.3 us
    pallas_call x2, Pallas kernels, up_project(): pl.pallas_call(functools.partial(up_kernel, len(parts), len(gate_parts),...  18.8 us
    pallas_call x2, Pallas kernels, down_project(): pl.pallas_call(down_kernel, grid=(STEPS,), out_shape=[jax.ShapeDtypeStruc...  16.6 us
    reshape x4, local copies, waits for them, and re-layouts, to_nodes(): pieces = value.reshape(nodes, rows // nodes, 2, width // 2)  6.23 us
  transfers between devices with their start and end apart: 24, of which 12 were waited for; matrix products, arithmetic and copies ran while one was open for 4% of the time, Pallas kernels for 14%

profile of v2, /device:TPU:1, one launch (start us, length us, event | category | flops | bytes accessed | tf_op | source)
XLA Modules:
  0.0 250.4 jit_solution(1481943235723870922)
XLA Ops:
  0.0 1.1 copy-done
  1.1 0.7 copy-done.1
  1.8 0.7 copy-done.2
  2.5 0.7 copy-done.3
  3.1 1.2 select.1
  4.3 1.7 reshape.27
  6.0 9.4 %all-to-all-start.2 = ((bf16[32,3,2,2560]{3,2,1,0:T(2,128)(2,1)}), bf16[32,3,2,2560]{3,2,1,0:T(2,128)(2,1)S(1)}, u32[]{:S(2)}, u32[]{:S(2)}) async-start(bf16[32,3,2,2560]{3,2,1,0:T(2,128)(2,1)} %reshape.27), calls=%async_computation.2 | async-start | bytes 1966080 | tf_op jit(solution)/shard_map/all_to_all | solution.py:201
  15.4 1.2 reshape.24
  16.7 15.0 %all-to-all-done.2 = bf16[32,3,2,2560]{3,2,1,0:T(2,128)(2,1)S(1)} async-done(((bf16[32,3,2,2560]{3,2,1,0:T(2,128)(2,1)}), bf16[32,3,2,2560]{3,2,1,0:T(2,128)(2,1)S(1)}, u32[]{:S(2)}, u32[]{:S(2)}) %all-to-all-start.2) | async-done | bytes 983072 | tf_op jit(solution)/shard_map/all_to_all | solution.py:201
  31.6 4.4 %all-to-all-start = ((bf16[32,3,2,2688]{3,2,1,0:T(2,128)(2,1)}), bf16[32,3,2,2688]{3,2,1,0:T(2,128)(2,1)}, u32[]{:S(2)}, u32[]{:S(2)}) async-start(bf16[32,3,2,2688]{3,2,1,0:T(2,128)(2,1)} %reshape.24), calls=%async_computation | async-start | bytes 2064384 | tf_op jit(solution)/shard_map/all_to_all | solution.py:201
  36.2 2.8 %collective-permute-start.11 = (bf16[96,5120]{1,0:T(8,128)(2,1)S(1)}, bf16[96,5120]{1,0:T(8,128)(2,1)S(1)}, u32[]{:S(2)}, u32[]{:S(2)}) collective-permute-start(bf16[96,5120]{1,0:T(8,128)(2,1)S(1)} %bitcast.29), channel_id=1, source_target_pairs={{0,3},{1,0},{2,1},{3,2},{4,7},{5,4},{6,5},{7,6},{8,11},{9,8},{10,9... | collective-permute-start | bytes 2949128 | tf_op jit(solution)/shard_map/ppermute | solution.py:195
  39.0 13.8 %all-to-all-done = bf16[32,3,2,2688]{3,2,1,0:T(2,128)(2,1)} async-done(((bf16[32,3,2,2688]{3,2,1,0:T(2,128)(2,1)}), bf16[32,3,2,2688]{3,2,1,0:T(2,128)(2,1)}, u32[]{:S(2)}, u32[]{:S(2)}) %all-to-all-start) | async-done | bytes 1032224 | tf_op jit(solution)/shard_map/all_to_all | solution.py:201
  52.8 1.9 fusion.4
  54.9 1.4 collective-permute-start
  56.2 1.5 collective-permute-start.3
  57.8 2.7 %collective-permute-start.2 = (bf16[48,5376]{1,0:T(8,128)(2,1)S(1)}, bf16[48,5376]{1,0:T(8,128)(2,1)S(1)}, u32[]{:S(2)}, u32[]{:S(2)}) collective-permute-start(bf16[48,5376]{1,0:T(8,128)(2,1)S(1)} %bitcast.25), channel_id=1, source_target_pairs={{0,3},{1,0},{2,1},{3,2},{4,7},{5,4},{6,5},{7,6},{8,11},{9,8},{10,9... | collective-permute-start | bytes 1548296 | tf_op jit(solution)/shard_map/ppermute | solution.py:195
  60.4 9.1 %collective-permute-done.refs_2_.refs_10_.refs_7_ = bf16[48,5376]{1,0:T(8,128)(2,1)S(1)} collective-permute-done((bf16[48,5376]{1,0:T(8,128)(2,1)S(1)}, bf16[48,5376]{1,0:T(8,128)(2,1)S(1)}, u32[]{:S(2)}, u32[]{:S(2)}) %collective-permute-start) | collective-permute-done | bytes 516128 | tf_op jit(solution)/shard_map/ppermute | solution.py:195
  69.5 1.4 collective-permute-done.3.refs_5_.refs_13_.refs_10_
  70.9 0.8 collective-permute-start.4
  71.7 2.7 %collective-permute-start.5 = (bf16[48,5376]{1,0:T(8,128)(2,1)S(1)}, bf16[48,5376]{1,0:T(8,128)(2,1)S(1)}, u32[]{:S(2)}, u32[]{:S(2)}) collective-permute-start(bf16[48,5376]{1,0:T(8,128)(2,1)S(1)} %collective-permute-done.3.refs_5_.refs_13_.refs_10_), channel_id=1, source_target_pairs={{0,3},{1,0},{2,1},{3,2},{4,7},{5,4},{6,5},{7,6},{8,11},{9,8},{10,9... | collective-permute-start | bytes 1548296 | tf_op jit(solution)/shard_map/ppermute | solution.py:195
  74.4 16.2 %collective-permute-done.10.refs_1_ = bf16[96,5120]{1,0:T(8,128)(2,1)S(1)} collective-permute-done((bf16[96,5120]{1,0:T(8,128)(2,1)S(1)}, bf16[96,5120]{1,0:T(8,128)(2,1)S(1)}, u32[]{:S(2)}, u32[]{:S(2)}) %collective-permute-start.10) | collective-permute-done | bytes 983072 | tf_op jit(solution)/shard_map/ppermute | solution.py:195
  90.6 1.4 collective-permute-start.13
  92.1 9.5 %collective-permute-done.1.refs_3_.refs_11_.refs_8_ = bf16[48,5376]{1,0:T(8,128)(2,1)S(1)} collective-permute-done((bf16[48,5376]{1,0:T(8,128)(2,1)S(1)}, bf16[48,5376]{1,0:T(8,128)(2,1)S(1)}, u32[]{:S(2)}, u32[]{:S(2)}) %collective-permute-start.1) | collective-permute-done | bytes 516128 | tf_op jit(solution)/shard_map/ppermute | solution.py:195
  101.6 11.1 %collective-permute-done.4.refs_6_.refs_14_.refs_11_ = bf16[48,5376]{1,0:T(8,128)(2,1)S(1)} collective-permute-done((bf16[48,5376]{1,0:T(8,128)(2,1)S(1)}, bf16[48,5376]{1,0:T(8,128)(2,1)S(1)}, u32[]{:S(2)}, u32[]{:S(2)}) %collective-permute-start.4) | collective-permute-done | bytes 516128 | tf_op jit(solution)/shard_map/ppermute | solution.py:195
  112.7 9.4 %up.2.hid = bf16[384,1152]{1,0:T(8,128)(2,1)S(1)} custom-call(bf16[48,5376]{1,0:T(8,128)(2,1)S(1)} %bitcast.26, bf16[48,5376]{1,0:T(8,128)(2,1)S(1)} %bitcast.21, bf16[48,5376]{1,0:T(8,128)(2,1)S(1)} %collective-permute-done.refs_2_.refs_10_.refs_7_, bf16[48,5376]{1,0:T(8,128)(2,1)S(1)} %collective-permute-done.1.refs_3_.refs_11_.refs_8_, ...), custom_call_target="tpu_custom_call" | custom-call | flops 4529848320 | bytes 16613376 | tf_op jit(solution)/shard_map/up/pallas_call | solution.py:149
  122.1 8.3 %down.4 = (bf16[96,5120]{1,0:T(8,128)(2,1)S(1)}, bf16[96,5120]{1,0:T(8,128)(2,1)S(1)}, bf16[96,5120]{1,0:T(8,128)(2,1)S(1)}, bf16[48,5120]{1,0:T(8,128)(2,1)S(1)}, bf16[48,5120]{1,0:T(8,128)(2,1)S(1)}) custom-call(bf16[384,1152]{1,0:T(8,128)(2,1)S(1)} %up.2.hid, bf16[3,384,5120]{2,1,0:T(8,128)(2,1)} %down.7), custom_call_target="tpu_custom_call" | custom-call | flops 4529848320 | bytes 16613376 | tf_op jit(solution)/shard_map/down/pallas_call | solution.py:178
  130.5 2.7 %collective-permute-start.8 = (bf16[48,5120]{1,0:T(8,128)(2,1)S(1)}, bf16[48,5120]{1,0:T(8,128)(2,1)S(1)}, u32[]{:S(2)}, u32[]{:S(2)}) collective-permute-start(bf16[48,5120]{1,0:T(8,128)(2,1)S(1)} %get-tuple-element.24), channel_id=1, source_target_pairs={{0,3},{1,0},{2,1},{3,2},{4,7},{5,4},{6,5},{7,6},{8,11},{9,8},{10,9... | collective-permute-start | bytes 1474568 | tf_op jit(solution)/shard_map/ppermute | solution.py:195
  133.2 9.4 %up.3.hid = bf16[384,1152]{1,0:T(8,128)(2,1)S(1)} custom-call(bf16[96,5120]{1,0:T(8,128)(2,1)S(1)} %bitcast.31, bf16[96,5120]{1,0:T(8,128)(2,1)S(1)} %collective-permute-done.10.refs_1_, bf16[96,5120]{1,0:T(8,128)(2,1)S(1)} %collective-permute-done.11.refs_2_, bf16[48,5120]{1,0:T(8,128)(2,1)S(1)} %collective-permute-done.12.refs_3_, ...), custom_call_target="tpu_custom_call" | custom-call | flops 4529848320 | bytes 16613376 | tf_op jit(solution)/shard_map/up/pallas_call | solution.py:149
  142.6 8.3 %down.6 = (bf16[96,5120]{1,0:T(8,128)(2,1)S(1)}, bf16[96,5120]{1,0:T(8,128)(2,1)S(1)}, bf16[96,5120]{1,0:T(8,128)(2,1)S(1)}, bf16[48,5120]{1,0:T(8,128)(2,1)S(1)}, bf16[48,5120]{1,0:T(8,128)(2,1)S(1)}) custom-call(bf16[384,1152]{1,0:T(8,128)(2,1)S(1)} %up.3.hid, bf16[3,384,5120]{2,1,0:T(8,128)(2,1)} %down.7), custom_call_target="tpu_custom_call" | custom-call | flops 4529848320 | bytes 16613376 | tf_op jit(solution)/shard_map/down/pallas_call | solution.py:178
  151.0 0.3 collective-permute-start.16
  151.2 1.3 collective-permute-start.17
  152.5 2.7 %collective-permute-start.18 = (bf16[48,5120]{1,0:T(8,128)(2,1)S(1)}, bf16[48,5120]{1,0:T(8,128)(2,1)S(1)}, u32[]{:S(2)}, u32[]{:S(2)}) collective-permute-start(bf16[48,5120]{1,0:T(8,128)(2,1)S(1)} %get-tuple-element.30), channel_id=1, source_target_pairs={{0,3},{1,0},{2,1},{3,2},{4,7},{5,4},{6,5},{7,6},{8,11},{9,8},{10,9... | collective-permute-start | bytes 1474568 | tf_op jit(solution)/shard_map/ppermute | solution.py:195
  155.4 0.3 collective-permute-start.9
  155.7 17.6 %collective-permute-done.14 = bf16[48,5120]{1,0:T(8,128)(2,1)S(1)} collective-permute-done((bf16[48,5120]{1,0:T(8,128)(2,1)S(1)}, bf16[48,5120]{1,0:T(8,128)(2,1)S(1)}, u32[]{:S(2)}, u32[]{:S(2)}) %collective-permute-start.14) | collective-permute-done | bytes 491552 | tf_op jit(solution)/shard_map/ppermute | solution.py:195
  173.5 0.3 collective-permute-start.15
  173.9 2.5 %collective-permute-start.19 = (bf16[48,5120]{1,0:T(8,128)(2,1)S(1)}, bf16[48,5120]{1,0:T(8,128)(2,1)S(1)}, u32[]{:S(2)}, u32[]{:S(2)}) collective-permute-start(bf16[48,5120]{1,0:T(8,128)(2,1)S(1)} %add_convert_fusion.2), channel_id=1, source_target_pairs={{0,3},{1,0},{2,1},{3,2},{4,7},{5,4},{6,5},{7,6},{8,11},{9,8},{10,9... | collective-permute-start | bytes 1474568 | tf_op jit(solution)/shard_map/ppermute | solution.py:195
  176.4 1.0 pad_maximum_fusion
  177.5 6.9 %collective-permute-done.15 = bf16[48,5120]{1,0:T(8,128)(2,1)S(1)} collective-permute-done((bf16[48,5120]{1,0:T(8,128)(2,1)S(1)}, bf16[48,5120]{1,0:T(8,128)(2,1)S(1)}, u32[]{:S(2)}, u32[]{:S(2)}) %collective-permute-start.15) | collective-permute-done | bytes 491552 | tf_op jit(solution)/shard_map/ppermute | solution.py:195
  184.4 19.7 %collective-permute-done.19 = bf16[48,5120]{1,0:T(8,128)(2,1)S(1)} collective-permute-done((bf16[48,5120]{1,0:T(8,128)(2,1)S(1)}, bf16[48,5120]{1,0:T(8,128)(2,1)S(1)}, u32[]{:S(2)}, u32[]{:S(2)}) %collective-permute-start.19) | collective-permute-done | bytes 491552 | tf_op jit(solution)/shard_map/ppermute | solution.py:195
  204.1 0.4 add_convert_fusion.3
  204.5 1.7 reshape.29
  206.2 6.3 %all-to-all-start.3 = ((bf16[32,3,2,2560]{3,2,1,0:T(2,128)(2,1)}), bf16[32,3,2,2560]{3,2,1,0:T(2,128)(2,1)S(1)}, u32[]{:S(2)}, u32[]{:S(2)}) async-start(bf16[32,3,2,2560]{3,2,1,0:T(2,128)(2,1)} %reshape.29), calls=%async_computation.3 | async-start | bytes 1966080 | tf_op jit(solution)/shard_map/all_to_all | solution.py:201
  212.5 1.9 add_convert_fusion
  214.4 1.7 reshape.25
  216.0 12.8 %all-to-all-done.3 = bf16[32,3,2,2560]{3,2,1,0:T(2,128)(2,1)S(1)} async-done(((bf16[32,3,2,2560]{3,2,1,0:T(2,128)(2,1)}), bf16[32,3,2,2560]{3,2,1,0:T(2,128)(2,1)S(1)}, u32[]{:S(2)}, u32[]{:S(2)}) %all-to-all-start.3) | async-done | bytes 983072 | tf_op jit(solution)/shard_map/all_to_all | solution.py:201
  228.8 3.9 %all-to-all-start.1 = ((bf16[32,3,2,2560]{3,2,1,0:T(2,128)(2,1)}), bf16[32,3,2,2560]{3,2,1,0:T(2,128)(2,1)S(1)}, u32[]{:S(2)}, u32[]{:S(2)}) async-start(bf16[32,3,2,2560]{3,2,1,0:T(2,128)(2,1)} %reshape.25), calls=%async_computation.1 | async-start | bytes 1966080 | tf_op jit(solution)/shard_map/all_to_all | solution.py:201
  232.8 16.1 %all-to-all-done.1 = bf16[32,3,2,2560]{3,2,1,0:T(2,128)(2,1)S(1)} async-done(((bf16[32,3,2,2560]{3,2,1,0:T(2,128)(2,1)}), bf16[32,3,2,2560]{3,2,1,0:T(2,128)(2,1)S(1)}, u32[]{:S(2)}, u32[]{:S(2)}) %all-to-all-start.1) | async-done | bytes 983072 | tf_op jit(solution)/shard_map/all_to_all | solution.py:201
  249.1 1.4 convolution_convert_fusion
  (39 shorter events, 1.5 us)
Async XLA Ops:
  0.0 1.1 copy-start
  1.1 0.7 copy-start.1
  1.8 0.7 copy-start.2
  2.5 0.7 copy-start.3
  6.0 25.7 %all-to-all-start.2 = ((bf16[32,3,2,2560]{3,2,1,0:T(2,128)(2,1)}), bf16[32,3,2,2560]{3,2,1,0:T(2,128)(2,1)S(1)}, u32[]{:S(2)}, u32[]{:S(2)}) async-start(bf16[32,3,2,2560]{3,2,1,0:T(2,128)(2,1)} %reshape.27), calls=%async_computation.2 | async-start | bytes 1966080 | tf_op jit(solution)/shard_map/all_to_all | solution.py:201
  31.6 21.2 %all-to-all-start = ((bf16[32,3,2,2688]{3,2,1,0:T(2,128)(2,1)}), bf16[32,3,2,2688]{3,2,1,0:T(2,128)(2,1)}, u32[]{:S(2)}, u32[]{:S(2)}) async-start(bf16[32,3,2,2688]{3,2,1,0:T(2,128)(2,1)} %reshape.24), calls=%async_computation | async-start | bytes 2064384 | tf_op jit(solution)/shard_map/all_to_all | solution.py:201
  36.2 35.5 %collective-permute-start.11 = (bf16[96,5120]{1,0:T(8,128)(2,1)S(1)}, bf16[96,5120]{1,0:T(8,128)(2,1)S(1)}, u32[]{:S(2)}, u32[]{:S(2)}) collective-permute-start(bf16[96,5120]{1,0:T(8,128)(2,1)S(1)} %bitcast.29), channel_id=1, source_target_pairs={{0,3},{1,0},{2,1},{3,2},{4,7},{5,4},{6,5},{7,6},{8,11},{9,8},{10,9... | collective-permute-start | bytes 2949128 | tf_op jit(solution)/shard_map/ppermute | solution.py:195
  54.9 14.6 %collective-permute-start = (bf16[48,5376]{1,0:T(8,128)(2,1)S(1)}, bf16[48,5376]{1,0:T(8,128)(2,1)S(1)}, u32[]{:S(2)}, u32[]{:S(2)}) collective-permute-start(bf16[48,5376]{1,0:T(8,128)(2,1)S(1)} %bitcast.24), channel_id=1, source_target_pairs={{0,1},{1,2},{2,3},{3,0},{4,5},{5,6},{6,7},{7,4},{8,9},{9,10},{10,1... | collective-permute-start | bytes 1548296 | tf_op jit(solution)/shard_map/ppermute | solution.py:195
  56.2 14.7 %collective-permute-start.3 = (bf16[48,5376]{1,0:T(8,128)(2,1)S(1)}, bf16[48,5376]{1,0:T(8,128)(2,1)S(1)}, u32[]{:S(2)}, u32[]{:S(2)}) collective-permute-start(bf16[48,5376]{1,0:T(8,128)(2,1)S(1)} %bitcast.19), channel_id=1, source_target_pairs={{0,3},{1,0},{2,1},{3,2},{4,7},{5,4},{6,5},{7,6},{8,11},{9,8},{10,9... | collective-permute-start | bytes 1548296 | tf_op jit(solution)/shard_map/ppermute | solution.py:195
  57.8 32.8 %collective-permute-start.10 = (bf16[96,5120]{1,0:T(8,128)(2,1)S(1)}, bf16[96,5120]{1,0:T(8,128)(2,1)S(1)}, u32[]{:S(2)}, u32[]{:S(2)}) collective-permute-start(bf16[96,5120]{1,0:T(8,128)(2,1)S(1)} %bitcast.30), channel_id=1, source_target_pairs={{0,1},{1,2},{2,3},{3,0},{4,5},{5,6},{6,7},{7,4},{8,9},{9,10},{10,1... | collective-permute-start | bytes 2949128 | tf_op jit(solution)/shard_map/ppermute | solution.py:195
  57.8 34.2 %collective-permute-start.2 = (bf16[48,5376]{1,0:T(8,128)(2,1)S(1)}, bf16[48,5376]{1,0:T(8,128)(2,1)S(1)}, u32[]{:S(2)}, u32[]{:S(2)}) collective-permute-start(bf16[48,5376]{1,0:T(8,128)(2,1)S(1)} %bitcast.25), channel_id=1, source_target_pairs={{0,3},{1,0},{2,1},{3,2},{4,7},{5,4},{6,5},{7,6},{8,11},{9,8},{10,9... | collective-permute-start | bytes 1548296 | tf_op jit(solution)/shard_map/ppermute | solution.py:195
  69.5 32.1 %collective-permute-start.1 = (bf16[48,5376]{1,0:T(8,128)(2,1)S(1)}, bf16[48,5376]{1,0:T(8,128)(2,1)S(1)}, u32[]{:S(2)}, u32[]{:S(2)}) collective-permute-start(bf16[48,5376]{1,0:T(8,128)(2,1)S(1)} %bitcast.20), channel_id=1, source_target_pairs={{0,1},{1,2},{2,3},{3,0},{4,5},{5,6},{6,7},{7,4},{8,9},{9,10},{10,1... | collective-permute-start | bytes 1548296 | tf_op jit(solution)/shard_map/ppermute | solution.py:195
  70.9 41.8 %collective-permute-start.4 = (bf16[48,5376]{1,0:T(8,128)(2,1)S(1)}, bf16[48,5376]{1,0:T(8,128)(2,1)S(1)}, u32[]{:S(2)}, u32[]{:S(2)}) collective-permute-start(bf16[48,5376]{1,0:T(8,128)(2,1)S(1)} %collective-permute-done.refs_2_.refs_10_.refs_7_), channel_id=1, source_target_pairs={{0,1},{1,2},{2,3},{3,0},{4,5},{5,6},{6,7},{7,4},{8,9},{9,10},{10,1... | collective-permute-start | bytes 1548296 | tf_op jit(solution)/shard_map/ppermute | solution.py:195
  71.7 41.0 %collective-permute-start.5 = (bf16[48,5376]{1,0:T(8,128)(2,1)S(1)}, bf16[48,5376]{1,0:T(8,128)(2,1)S(1)}, u32[]{:S(2)}, u32[]{:S(2)}) collective-permute-start(bf16[48,5376]{1,0:T(8,128)(2,1)S(1)} %collective-permute-done.3.refs_5_.refs_13_.refs_10_), channel_id=1, source_target_pairs={{0,3},{1,0},{2,1},{3,2},{4,7},{5,4},{6,5},{7,6},{8,11},{9,8},{10,9... | collective-permute-start | bytes 1548296 | tf_op jit(solution)/shard_map/ppermute | solution.py:195
  90.6 42.6 %collective-permute-start.13 = (bf16[48,5120]{1,0:T(8,128)(2,1)S(1)}, bf16[48,5120]{1,0:T(8,128)(2,1)S(1)}, u32[]{:S(2)}, u32[]{:S(2)}) collective-permute-start(bf16[48,5120]{1,0:T(8,128)(2,1)S(1)} %slice.67), channel_id=1, source_target_pairs={{0,3},{1,0},{2,1},{3,2},{4,7},{5,4},{6,5},{7,6},{8,11},{9,8},{10,9... | collective-permute-start | bytes 1474568 | tf_op jit(solution)/shard_map/ppermute | solution.py:195
  92.0 41.2 %collective-permute-start.12 = (bf16[48,5120]{1,0:T(8,128)(2,1)S(1)}, bf16[48,5120]{1,0:T(8,128)(2,1)S(1)}, u32[]{:S(2)}, u32[]{:S(2)}) collective-permute-start(bf16[48,5120]{1,0:T(8,128)(2,1)S(1)} %slice.66), channel_id=1, source_target_pairs={{0,1},{1,2},{2,3},{3,0},{4,5},{5,6},{6,7},{7,4},{8,9},{9,10},{10,1... | collective-permute-start | bytes 1474568 | tf_op jit(solution)/shard_map/ppermute | solution.py:195
  130.4 24.9 %collective-permute-start.6 = (bf16[48,5120]{1,0:T(8,128)(2,1)S(1)}, bf16[48,5120]{1,0:T(8,128)(2,1)S(1)}, u32[]{:S(2)}, u32[]{:S(2)}) collective-permute-start(bf16[48,5120]{1,0:T(8,128)(2,1)S(1)} %get-tuple-element.22), channel_id=1, source_target_pairs={{0,1},{1,2},{2,3},{3,0},{4,5},{5,6},{6,7},{7,4},{8,9},{9,10},{10,1... | collective-permute-start | bytes 1474568 | tf_op jit(solution)/shard_map/ppermute | solution.py:195
  130.5 22.0 %collective-permute-start.8 = (bf16[48,5120]{1,0:T(8,128)(2,1)S(1)}, bf16[48,5120]{1,0:T(8,128)(2,1)S(1)}, u32[]{:S(2)}, u32[]{:S(2)}) collective-permute-start(bf16[48,5120]{1,0:T(8,128)(2,1)S(1)} %get-tuple-element.24), channel_id=1, source_target_pairs={{0,3},{1,0},{2,1},{3,2},{4,7},{5,4},{6,5},{7,6},{8,11},{9,8},{10,9... | collective-permute-start | bytes 1474568 | tf_op jit(solution)/shard_map/ppermute | solution.py:195
  151.0 26.5 %collective-permute-start.16 = (bf16[48,5120]{1,0:T(8,128)(2,1)S(1)}, bf16[48,5120]{1,0:T(8,128)(2,1)S(1)}, u32[]{:S(2)}, u32[]{:S(2)}) collective-permute-start(bf16[48,5120]{1,0:T(8,128)(2,1)S(1)} %slice.60), channel_id=1, source_target_pairs={{0,3},{1,0},{2,1},{3,2},{4,7},{5,4},{6,5},{7,6},{8,11},{9,8},{10,9... | collective-permute-start | bytes 1474568 | tf_op jit(solution)/shard_map/ppermute | solution.py:195
  151.2 26.3 %collective-permute-start.17 = (bf16[48,5120]{1,0:T(8,128)(2,1)S(1)}, bf16[48,5120]{1,0:T(8,128)(2,1)S(1)}, u32[]{:S(2)}, u32[]{:S(2)}) collective-permute-start(bf16[48,5120]{1,0:T(8,128)(2,1)S(1)} %slice.62), channel_id=1, source_target_pairs={{0,1},{1,2},{2,3},{3,0},{4,5},{5,6},{6,7},{7,4},{8,9},{9,10},{10,1... | collective-permute-start | bytes 1474568 | tf_op jit(solution)/shard_map/ppermute | solution.py:195
  152.5 20.9 %collective-permute-start.14 = (bf16[48,5120]{1,0:T(8,128)(2,1)S(1)}, bf16[48,5120]{1,0:T(8,128)(2,1)S(1)}, u32[]{:S(2)}, u32[]{:S(2)}) collective-permute-start(bf16[48,5120]{1,0:T(8,128)(2,1)S(1)} %get-tuple-element.28), channel_id=1, source_target_pairs={{0,1},{1,2},{2,3},{3,0},{4,5},{5,6},{6,7},{7,4},{8,9},{9,10},{10,1... | collective-permute-start | bytes 1474568 | tf_op jit(solution)/shard_map/ppermute | solution.py:195
  152.5 21.3 %collective-permute-start.18 = (bf16[48,5120]{1,0:T(8,128)(2,1)S(1)}, bf16[48,5120]{1,0:T(8,128)(2,1)S(1)}, u32[]{:S(2)}, u32[]{:S(2)}) collective-permute-start(bf16[48,5120]{1,0:T(8,128)(2,1)S(1)} %get-tuple-element.30), channel_id=1, source_target_pairs={{0,3},{1,0},{2,1},{3,2},{4,7},{5,4},{6,5},{7,6},{8,11},{9,8},{10,9... | collective-permute-start | bytes 1474568 | tf_op jit(solution)/shard_map/ppermute | solution.py:195
  155.4 57.1 %collective-permute-start.9 = (bf16[96,5120]{1,0:T(8,128)(2,1)S(1)}, bf16[96,5120]{1,0:T(8,128)(2,1)}, u32[]{:S(2)}, u32[]{:S(2)}) collective-permute-start(bf16[96,5120]{1,0:T(8,128)(2,1)S(1)} %pad_maximum_fusion.1), channel_id=1, source_target_pairs={{0,3},{1,0},{2,1},{3,2},{4,7},{5,4},{6,5},{7,6},{8,11},{9,8},{10,9... | collective-permute-start | bytes 2949128 | tf_op jit(solution)/shard_map/ppermute | solution.py:195
  173.5 10.9 %collective-permute-start.15 = (bf16[48,5120]{1,0:T(8,128)(2,1)S(1)}, bf16[48,5120]{1,0:T(8,128)(2,1)S(1)}, u32[]{:S(2)}, u32[]{:S(2)}) collective-permute-start(bf16[48,5120]{1,0:T(8,128)(2,1)S(1)} %add_convert_fusion.4), channel_id=1, source_target_pairs={{0,1},{1,2},{2,3},{3,0},{4,5},{5,6},{6,7},{7,4},{8,9},{9,10},{10,1... | collective-permute-start | bytes 1474568 | tf_op jit(solution)/shard_map/ppermute | solution.py:195
  173.9 30.2 %collective-permute-start.19 = (bf16[48,5120]{1,0:T(8,128)(2,1)S(1)}, bf16[48,5120]{1,0:T(8,128)(2,1)S(1)}, u32[]{:S(2)}, u32[]{:S(2)}) collective-permute-start(bf16[48,5120]{1,0:T(8,128)(2,1)S(1)} %add_convert_fusion.2), channel_id=1, source_target_pairs={{0,3},{1,0},{2,1},{3,2},{4,7},{5,4},{6,5},{7,6},{8,11},{9,8},{10,9... | collective-permute-start | bytes 1474568 | tf_op jit(solution)/shard_map/ppermute | solution.py:195
  177.5 35.0 %collective-permute-start.7 = (bf16[96,5120]{1,0:T(8,128)(2,1)}, bf16[96,5120]{1,0:T(8,128)(2,1)}, u32[]{:S(2)}, u32[]{:S(2)}) collective-permute-start(bf16[96,5120]{1,0:T(8,128)(2,1)} %pad_maximum_fusion), channel_id=1, source_target_pairs={{0,1},{1,2},{2,3},{3,0},{4,5},{5,6},{6,7},{7,4},{8,9},{9,10},{10,1... | collective-permute-start | bytes 2949128 | tf_op jit(solution)/shard_map/ppermute | solution.py:195
  206.2 22.6 %all-to-all-start.3 = ((bf16[32,3,2,2560]{3,2,1,0:T(2,128)(2,1)}), bf16[32,3,2,2560]{3,2,1,0:T(2,128)(2,1)S(1)}, u32[]{:S(2)}, u32[]{:S(2)}) async-start(bf16[32,3,2,2560]{3,2,1,0:T(2,128)(2,1)} %reshape.29), calls=%async_computation.3 | async-start | bytes 1966080 | tf_op jit(solution)/shard_map/all_to_all | solution.py:201
  228.8 20.1 %all-to-all-start.1 = ((bf16[32,3,2,2560]{3,2,1,0:T(2,128)(2,1)}), bf16[32,3,2,2560]{3,2,1,0:T(2,128)(2,1)S(1)}, u32[]{:S(2)}, u32[]{:S(2)}) async-start(bf16[32,3,2,2560]{3,2,1,0:T(2,128)(2,1)} %reshape.25), calls=%async_computation.1 | async-start | bytes 1966080 | tf_op jit(solution)/shard_map/all_to_all | solution.py:201

commit v3 on v2

--- a/solution.py
+++ b/solution.py
@@ -216,37 +216,25 @@
     )
     half = groups[0].shape[0] // 2
     gathered = []
-    for g, sent in enumerate(groups):
+    for sent in groups:
         own = to_nodes(sent, nodes)
-        if g == 0:
-            top, low = own[:half], own[half:]
-            right_top, left_low = shift(top, 1), shift(low, -1)
-            right_low, left_top = shift(low, 1), shift(top, -1)
-            far_a, far_b = shift(right_top, 1), shift(left_low, -1)
-            parts = (top, low, right_top, right_low, left_top, left_low, far_a, far_b)
-        else:
-            right, left = shift(own, 1), shift(own, -1)
-            far_a, far_b = shift(right[:half], 1), shift(left[half:], -1)
-            parts = (own, right, left, far_a, far_b)
+        top, low = own[:half], own[half:]
+        right_top, left_low = shift(top, 1), shift(low, -1)
+        right_low, left_top = shift(low, 1), shift(top, -1)
+        far_a, far_b = shift(right_top, 1), shift(left_low, -1)
+        parts = (top, low, right_top, right_low, left_top, left_low, far_a, far_b)
         gathered.append(parts)
     returned = []
     for g, parts in enumerate(gathered):
         hid = up_project(parts, gathered[0], g * up_weight.shape[0], up_weight)
         own, right, left, far_a, far_b = down_project(hid, down_weight, [2 * half] * 3 + [half] * 2)
         in_a, in_b = shift(far_a, 1), shift(far_b, -1)
-        late_left, late_right = left[half:], right[:half]
-        if g == len(gathered) - 1:
-            late_left, late_right = shift(late_left, 1), shift(late_right, -1)
-            soon_left = shift(add(left[:half], in_a), 1)
-            soon_right = shift(add(right[half:], in_b), -1)
-            total = jnp.concatenate(
-                [add(own[:half], soon_left, late_right), add(own[half:], late_left, soon_right)],
-                axis=0,
-            )
-        else:
-            left = jnp.concatenate([add(left[:half], in_a), late_left], axis=0)
-            right = jnp.concatenate([late_right, add(right[half:], in_b)], axis=0)
-            total = add(own, shift(left, 1), shift(right, -1))
+        late_left, late_right = shift(left[half:], 1), shift(right[:half], -1)
+        soon_left = shift(add(left[:half], in_a), 1)
+        soon_right = shift(add(right[half:], in_b), -1)
+        total = jnp.concatenate(
+            [add(own[:half], soon_left, late_right), add(own[half:], late_left, soon_right)], axis=0
+        )
         returned.append(to_nodes(total, nodes))
     combined = lax.dot_general(
         place,

time: 251 us -> 218 us (0.87)
  waiting for transfers between devices: 149 us -> 105 us
  starting transfers between devices: 47.4 us -> 58.1 us
    ppermute x20 -> x24, waiting for transfers between devices: 91.5 us -> 48.5 us  [shift(): lax.ppermute(value, 'local', [(i, (i + by) % size) for i in range(size)])]
    all_to_all x4, starting transfers between devices: 24 us -> 29.9 us  [to_nodes(): lax.all_to_all(pieces, 'node', split_axis=0, concat_axis=0, tiled=True)]
    ppermute x20 -> x24, starting transfers between devices: 23.3 us -> 28.2 us  [shift(): lax.ppermute(value, 'local', [(i, (i + by) % size) for i in range(size)])]
  transfers between devices with their start and end apart: 24 -> 28, of which waited for: 12 -> 11; matrix products, arithmetic and copies ran while one was open for 4% -> 5% of each run, Pallas kernels for 14% -> 16%
where the time goes in v3:
time: 218 us; the launch traced here: 217 us
  waiting for transfers between devices  105 us (48%)
  starting transfers between devices  58.1 us (27%)
  Pallas kernels  36.5 us (17%)
  local copies, waits for them, and re-layouts  11.3 us (5%)
  other arithmetic  4.19 us (2%)
    all_to_all x4, waiting for transfers between devices, to_nodes(): lax.all_to_all(pieces, 'node', split_axis=0, concat_axis=0, tiled=True)  56.5 us
    ppermute x24, waiting for transfers between devices, shift(): lax.ppermute(value, 'local', [(i, (i + by) % size) for i in range(size)])  48.5 us
    all_to_all x4, starting transfers between devices, to_nodes(): lax.all_to_all(pieces, 'node', split_axis=0, concat_axis=0, tiled=True)  29.9 us
    ppermute x24, starting transfers between devices, shift(): lax.ppermute(value, 'local', [(i, (i + by) % size) for i in range(size)])  28.2 us
    pallas_call x2, Pallas kernels, up_project(): pl.pallas_call(functools.partial(up_kernel, len(parts), len(gate_parts),...  18.8 us
    pallas_call x2, Pallas kernels, down_project(): pl.pallas_call(down_kernel, grid=(STEPS,), out_shape=[jax.ShapeDtypeStruc...  16.6 us
    reshape x4, local copies, waits for them, and re-layouts, to_nodes(): pieces = value.reshape(nodes, rows // nodes, 2, width // 2)  6.23 us
  transfers between devices with their start and end apart: 28, of which 11 were waited for; matrix products, arithmetic and copies ran while one was open for 5% of the time, Pallas kernels for 16%

profile of v3, /device:TPU:1, one launch (start us, length us, event | category | flops | bytes accessed | tf_op | source)
XLA Modules:
  0.0 216.8 jit_solution(18402962765279734228)
XLA Ops:
  0.0 1.1 copy-done
  1.1 0.7 copy-done.1
  1.8 0.7 copy-done.2
  2.5 0.7 copy-done.3
  3.1 1.2 select.1
  4.3 1.2 reshape.24
  5.6 9.4 %all-to-all-start = ((bf16[32,3,2,2688]{3,2,1,0:T(2,128)(2,1)}), bf16[32,3,2,2688]{3,2,1,0:T(2,128)(2,1)S(1)}, u32[]{:S(2)}, u32[]{:S(2)}) async-start(bf16[32,3,2,2688]{3,2,1,0:T(2,128)(2,1)} %reshape.24), calls=%async_computation | async-start | bytes 2064384 | tf_op jit(solution)/shard_map/all_to_all | solution.py:201
  15.0 1.7 reshape.27
  16.7 15.1 %all-to-all-done = bf16[32,3,2,2688]{3,2,1,0:T(2,128)(2,1)S(1)} async-done(((bf16[32,3,2,2688]{3,2,1,0:T(2,128)(2,1)}), bf16[32,3,2,2688]{3,2,1,0:T(2,128)(2,1)S(1)}, u32[]{:S(2)}, u32[]{:S(2)}) %all-to-all-start) | async-done | bytes 1032224 | tf_op jit(solution)/shard_map/all_to_all | solution.py:201
  31.7 3.9 %all-to-all-start.2 = ((bf16[32,3,2,2560]{3,2,1,0:T(2,128)(2,1)}), bf16[32,3,2,2560]{3,2,1,0:T(2,128)(2,1)S(1)}, u32[]{:S(2)}, u32[]{:S(2)}) async-start(bf16[32,3,2,2560]{3,2,1,0:T(2,128)(2,1)} %reshape.27), calls=%async_computation.2 | async-start | bytes 1966080 | tf_op jit(solution)/shard_map/all_to_all | solution.py:201
  35.7 0.7 fusion.4
  36.5 1.4 collective-permute-start
  37.9 1.5 collective-permute-start.3
  39.4 12.5 %all-to-all-done.2 = bf16[32,3,2,2560]{3,2,1,0:T(2,128)(2,1)S(1)} async-done(((bf16[32,3,2,2560]{3,2,1,0:T(2,128)(2,1)}), bf16[32,3,2,2560]{3,2,1,0:T(2,128)(2,1)S(1)}, u32[]{:S(2)}, u32[]{:S(2)}) %all-to-all-start.2) | async-done | bytes 983072 | tf_op jit(solution)/shard_map/all_to_all | solution.py:201
  51.9 0.7 fusion.5
  52.6 1.4 collective-permute-start.12
  54.0 1.5 collective-permute-start.2
  55.5 1.2 collective-permute-start.4
  56.8 1.5 collective-permute-start.5
  58.3 8.4 %collective-permute-done.12.refs_2_ = bf16[48,5120]{1,0:T(8,128)(2,1)S(1)} collective-permute-done((bf16[48,5120]{1,0:T(8,128)(2,1)S(1)}, bf16[48,5120]{1,0:T(8,128)(2,1)S(1)}, u32[]{:S(2)}, u32[]{:S(2)}) %collective-permute-start.12) | collective-permute-done | bytes 491552 | tf_op jit(solution)/shard_map/ppermute | solution.py:195
  66.8 1.4 collective-permute-start.15
  68.2 20.4 %collective-permute-done.15.refs_5_ = bf16[48,5120]{1,0:T(8,128)(2,1)S(1)} collective-permute-done((bf16[48,5120]{1,0:T(8,128)(2,1)S(1)}, bf16[48,5120]{1,0:T(8,128)(2,1)S(1)}, u32[]{:S(2)}, u32[]{:S(2)}) %collective-permute-start.15) | collective-permute-done | bytes 491552 | tf_op jit(solution)/shard_map/ppermute | solution.py:195
  88.6 2.9 %collective-permute-start.14 = (bf16[48,5120]{1,0:T(8,128)(2,1)S(1)}, bf16[48,5120]{1,0:T(8,128)(2,1)S(1)}, u32[]{:S(2)}, u32[]{:S(2)}) collective-permute-start(bf16[48,5120]{1,0:T(8,128)(2,1)S(1)} %bitcast.33), channel_id=1, source_target_pairs={{0,3},{1,0},{2,1},{3,2},{4,7},{5,4},{6,5},{7,6},{8,11},{9,8},{10,9... | collective-permute-start | bytes 1474568 | tf_op jit(solution)/shard_map/ppermute | solution.py:195
  91.5 2.8 %collective-permute-start.17 = (bf16[48,5120]{1,0:T(8,128)(2,1)S(1)}, bf16[48,5120]{1,0:T(8,128)(2,1)S(1)}, u32[]{:S(2)}, u32[]{:S(2)}) collective-permute-start(bf16[48,5120]{1,0:T(8,128)(2,1)S(1)} %collective-permute-done.15.refs_5_), channel_id=1, source_target_pairs={{0,3},{1,0},{2,1},{3,2},{4,7},{5,4},{6,5},{7,6},{8,11},{9,8},{10,9... | collective-permute-start | bytes 1474568 | tf_op jit(solution)/shard_map/ppermute | solution.py:195
  94.4 9.4 %up.2.hid = bf16[384,1152]{1,0:T(8,128)(2,1)S(1)} custom-call(bf16[48,5376]{1,0:T(8,128)(2,1)S(1)} %bitcast.29, bf16[48,5376]{1,0:T(8,128)(2,1)S(1)} %bitcast.24, bf16[48,5376]{1,0:T(8,128)(2,1)S(1)} %collective-permute-done.refs_2_.refs_10_, bf16[48,5376]{1,0:T(8,128)(2,1)S(1)} %collective-permute-done.1.refs_3_.refs_11_, ...), custom_call_target="tpu_custom_call" | custom-call | flops 4529848320 | bytes 16613376 | tf_op jit(solution)/shard_map/up/pallas_call | solution.py:149
  103.8 8.3 %down.4 = (bf16[96,5120]{1,0:T(8,128)(2,1)S(1)}, bf16[96,5120]{1,0:T(8,128)(2,1)S(1)}, bf16[96,5120]{1,0:T(8,128)(2,1)S(1)}, bf16[48,5120]{1,0:T(8,128)(2,1)S(1)}, bf16[48,5120]{1,0:T(8,128)(2,1)S(1)}) custom-call(bf16[384,1152]{1,0:T(8,128)(2,1)S(1)} %up.2.hid, bf16[3,384,5120]{2,1,0:T(8,128)(2,1)} %down.7), custom_call_target="tpu_custom_call" | custom-call | flops 4529848320 | bytes 16613376 | tf_op jit(solution)/shard_map/down/pallas_call | solution.py:178
  112.1 1.3 collective-permute-start.8
  113.8 0.9 collective-permute-done.16.refs_6_
  114.6 1.7 collective-permute-start.10
  116.4 9.4 %up.3.hid = bf16[384,1152]{1,0:T(8,128)(2,1)S(1)} custom-call(bf16[48,5120]{1,0:T(8,128)(2,1)S(1)} %bitcast.34, bf16[48,5120]{1,0:T(8,128)(2,1)S(1)} %bitcast.37, bf16[48,5120]{1,0:T(8,128)(2,1)S(1)} %collective-permute-done.12.refs_2_, bf16[48,5120]{1,0:T(8,128)(2,1)S(1)} %collective-permute-done.13.refs_3_, ...), custom_call_target="tpu_custom_call" | custom-call | flops 4529848320 | bytes 16613376 | tf_op jit(solution)/shard_map/up/pallas_call | solution.py:149
  125.7 8.3 %down.6 = (bf16[96,5120]{1,0:T(8,128)(2,1)S(1)}, bf16[96,5120]{1,0:T(8,128)(2,1)S(1)}, bf16[96,5120]{1,0:T(8,128)(2,1)S(1)}, bf16[48,5120]{1,0:T(8,128)(2,1)S(1)}, bf16[48,5120]{1,0:T(8,128)(2,1)S(1)}) custom-call(bf16[384,1152]{1,0:T(8,128)(2,1)S(1)} %up.3.hid, bf16[3,384,5120]{2,1,0:T(8,128)(2,1)} %down.7), custom_call_target="tpu_custom_call" | custom-call | flops 4529848320 | bytes 16613376 | tf_op jit(solution)/shard_map/down/pallas_call | solution.py:178
  134.1 1.3 collective-permute-start.20
  135.8 2.6 %collective-permute-start.22 = (bf16[48,5120]{1,0:T(8,128)(2,1)S(1)}, bf16[48,5120]{1,0:T(8,128)(2,1)S(1)}, u32[]{:S(2)}, u32[]{:S(2)}) collective-permute-start(bf16[48,5120]{1,0:T(8,128)(2,1)S(1)} %get-tuple-element.30), channel_id=1, source_target_pairs={{0,3},{1,0},{2,1},{3,2},{4,7},{5,4},{6,5},{7,6},{8,11},{9,8},{10,9... | collective-permute-start | bytes 1474568 | tf_op jit(solution)/shard_map/ppermute | solution.py:195
  138.5 7.5 %collective-permute-done.18 = bf16[48,5120]{1,0:T(8,128)(2,1)S(1)} collective-permute-done((bf16[48,5120]{1,0:T(8,128)(2,1)S(1)}, bf16[48,5120]{1,0:T(8,128)(2,1)S(1)}, u32[]{:S(2)}, u32[]{:S(2)}) %collective-permute-start.18) | collective-permute-done | bytes 491552 | tf_op jit(solution)/shard_map/ppermute | solution.py:195
  146.0 0.9 add_convert_fusion.3
  146.9 7.6 %collective-permute-done.22 = bf16[48,5120]{1,0:T(8,128)(2,1)S(1)} collective-permute-done((bf16[48,5120]{1,0:T(8,128)(2,1)S(1)}, bf16[48,5120]{1,0:T(8,128)(2,1)S(1)}, u32[]{:S(2)}, u32[]{:S(2)}) %collective-permute-start.22) | collective-permute-done | bytes 491552 | tf_op jit(solution)/shard_map/ppermute | solution.py:195
  154.5 2.2 collective-permute-start.11
  156.7 0.9 add_convert_fusion.1
  157.7 2.9 %collective-permute-start.23 = (bf16[48,5120]{1,0:T(8,128)(2,1)}, bf16[48,5120]{1,0:T(8,128)(2,1)}, u32[]{:S(2)}, u32[]{:S(2)}) collective-permute-start(bf16[48,5120]{1,0:T(8,128)(2,1)} %add_convert_fusion.1), channel_id=1, source_target_pairs={{0,3},{1,0},{2,1},{3,2},{4,7},{5,4},{6,5},{7,6},{8,11},{9,8},{10,9... | collective-permute-start | bytes 1474568 | tf_op jit(solution)/shard_map/ppermute | solution.py:195
  160.5 3.6 %collective-permute-done.11 = bf16[48,5120]{1,0:T(8,128)(2,1)S(1)} collective-permute-done((bf16[48,5120]{1,0:T(8,128)(2,1)S(1)}, bf16[48,5120]{1,0:T(8,128)(2,1)S(1)}, u32[]{:S(2)}, u32[]{:S(2)}) %collective-permute-start.11) | collective-permute-done | bytes 491552 | tf_op jit(solution)/shard_map/ppermute | solution.py:195
  164.6 1.7 reshape.25
  166.3 12.6 %all-to-all-start.1 = ((bf16[32,3,2,2560]{3,2,1,0:T(2,128)(2,1)}), bf16[32,3,2,2560]{3,2,1,0:T(2,128)(2,1)S(1)}, u32[]{:S(2)}, u32[]{:S(2)}) async-start(bf16[32,3,2,2560]{3,2,1,0:T(2,128)(2,1)} %reshape.25), calls=%async_computation.1 | async-start | bytes 1966080 | tf_op jit(solution)/shard_map/all_to_all | solution.py:201
  179.0 1.7 add_convert_fusion.2
  180.7 1.7 reshape.28
  182.4 12.9 %all-to-all-done.1 = bf16[32,3,2,2560]{3,2,1,0:T(2,128)(2,1)S(1)} async-done(((bf16[32,3,2,2560]{3,2,1,0:T(2,128)(2,1)}), bf16[32,3,2,2560]{3,2,1,0:T(2,128)(2,1)S(1)}, u32[]{:S(2)}, u32[]{:S(2)}) %all-to-all-start.1) | async-done | bytes 983072 | tf_op jit(solution)/shard_map/all_to_all | solution.py:201
  195.2 3.9 %all-to-all-start.3 = ((bf16[32,3,2,2560]{3,2,1,0:T(2,128)(2,1)}), bf16[32,3,2,2560]{3,2,1,0:T(2,128)(2,1)S(1)}, u32[]{:S(2)}, u32[]{:S(2)}) async-start(bf16[32,3,2,2560]{3,2,1,0:T(2,128)(2,1)} %reshape.28), calls=%async_computation.3 | async-start | bytes 1966080 | tf_op jit(solution)/shard_map/all_to_all | solution.py:201
  199.2 16.1 %all-to-all-done.3 = bf16[32,3,2,2560]{3,2,1,0:T(2,128)(2,1)S(1)} async-done(((bf16[32,3,2,2560]{3,2,1,0:T(2,128)(2,1)}), bf16[32,3,2,2560]{3,2,1,0:T(2,128)(2,1)S(1)}, u32[]{:S(2)}, u32[]{:S(2)}) %all-to-all-start.3) | async-done | bytes 983072 | tf_op jit(solution)/shard_map/all_to_all | solution.py:201
  215.5 1.4 convolution_convert_fusion
  (46 shorter events, 2.1 us)
Async XLA Ops:
  0.0 1.1 copy-start
  1.1 0.7 copy-start.1
  1.8 0.7 copy-start.2
  2.5 0.7 copy-start.3
  5.6 26.2 %all-to-all-start = ((bf16[32,3,2,2688]{3,2,1,0:T(2,128)(2,1)}), bf16[32,3,2,2688]{3,2,1,0:T(2,128)(2,1)S(1)}, u32[]{:S(2)}, u32[]{:S(2)}) async-start(bf16[32,3,2,2688]{3,2,1,0:T(2,128)(2,1)} %reshape.24), calls=%async_computation | async-start | bytes 2064384 | tf_op jit(solution)/shard_map/all_to_all | solution.py:201
  31.7 20.2 %all-to-all-start.2 = ((bf16[32,3,2,2560]{3,2,1,0:T(2,128)(2,1)}), bf16[32,3,2,2560]{3,2,1,0:T(2,128)(2,1)S(1)}, u32[]{:S(2)}, u32[]{:S(2)}) async-start(bf16[32,3,2,2560]{3,2,1,0:T(2,128)(2,1)} %reshape.27), calls=%async_computation.2 | async-start | bytes 1966080 | tf_op jit(solution)/shard_map/all_to_all | solution.py:201
  36.5 19.0 %collective-permute-start = (bf16[48,5376]{1,0:T(8,128)(2,1)S(1)}, bf16[48,5376]{1,0:T(8,128)(2,1)S(1)}, u32[]{:S(2)}, u32[]{:S(2)}) collective-permute-start(bf16[48,5376]{1,0:T(8,128)(2,1)S(1)} %bitcast.27), channel_id=1, source_target_pairs={{0,1},{1,2},{2,3},{3,0},{4,5},{5,6},{6,7},{7,4},{8,9},{9,10},{10,1... | collective-permute-start | bytes 1548296 | tf_op jit(solution)/shard_map/ppermute | solution.py:195
  37.9 18.9 %collective-permute-start.3 = (bf16[48,5376]{1,0:T(8,128)(2,1)S(1)}, bf16[48,5376]{1,0:T(8,128)(2,1)S(1)}, u32[]{:S(2)}, u32[]{:S(2)}) collective-permute-start(bf16[48,5376]{1,0:T(8,128)(2,1)S(1)} %bitcast.22), channel_id=1, source_target_pairs={{0,3},{1,0},{2,1},{3,2},{4,7},{5,4},{6,5},{7,6},{8,11},{9,8},{10,9... | collective-permute-start | bytes 1548296 | tf_op jit(solution)/shard_map/ppermute | solution.py:195
  52.6 14.1 %collective-permute-start.12 = (bf16[48,5120]{1,0:T(8,128)(2,1)S(1)}, bf16[48,5120]{1,0:T(8,128)(2,1)S(1)}, u32[]{:S(2)}, u32[]{:S(2)}) collective-permute-start(bf16[48,5120]{1,0:T(8,128)(2,1)S(1)} %bitcast.32), channel_id=1, source_target_pairs={{0,1},{1,2},{2,3},{3,0},{4,5},{5,6},{6,7},{7,4},{8,9},{9,10},{10,1... | collective-permute-start | bytes 1474568 | tf_op jit(solution)/shard_map/ppermute | solution.py:195
  54.0 37.4 %collective-permute-start.2 = (bf16[48,5376]{1,0:T(8,128)(2,1)S(1)}, bf16[48,5376]{1,0:T(8,128)(2,1)S(1)}, u32[]{:S(2)}, u32[]{:S(2)}) collective-permute-start(bf16[48,5376]{1,0:T(8,128)(2,1)S(1)} %bitcast.28), channel_id=1, source_target_pairs={{0,3},{1,0},{2,1},{3,2},{4,7},{5,4},{6,5},{7,6},{8,11},{9,8},{10,9... | collective-permute-start | bytes 1548296 | tf_op jit(solution)/shard_map/ppermute | solution.py:195
  55.5 35.9 %collective-permute-start.1 = (bf16[48,5376]{1,0:T(8,128)(2,1)S(1)}, bf16[48,5376]{1,0:T(8,128)(2,1)S(1)}, u32[]{:S(2)}, u32[]{:S(2)}) collective-permute-start(bf16[48,5376]{1,0:T(8,128)(2,1)S(1)} %bitcast.23), channel_id=1, source_target_pairs={{0,1},{1,2},{2,3},{3,0},{4,5},{5,6},{6,7},{7,4},{8,9},{9,10},{10,1... | collective-permute-start | bytes 1548296 | tf_op jit(solution)/shard_map/ppermute | solution.py:195
  55.5 36.0 %collective-permute-start.4 = (bf16[48,5376]{1,0:T(8,128)(2,1)S(1)}, bf16[48,5376]{1,0:T(8,128)(2,1)S(1)}, u32[]{:S(2)}, u32[]{:S(2)}) collective-permute-start(bf16[48,5376]{1,0:T(8,128)(2,1)S(1)} %collective-permute-done.refs_2_.refs_10_), channel_id=1, source_target_pairs={{0,1},{1,2},{2,3},{3,0},{4,5},{5,6},{6,7},{7,4},{8,9},{9,10},{10,1... | collective-permute-start | bytes 1548296 | tf_op jit(solution)/shard_map/ppermute | solution.py:195
  56.8 37.6 %collective-permute-start.5 = (bf16[48,5376]{1,0:T(8,128)(2,1)S(1)}, bf16[48,5376]{1,0:T(8,128)(2,1)S(1)}, u32[]{:S(2)}, u32[]{:S(2)}) collective-permute-start(bf16[48,5376]{1,0:T(8,128)(2,1)S(1)} %collective-permute-done.3.refs_5_.refs_13_), channel_id=1, source_target_pairs={{0,3},{1,0},{2,1},{3,2},{4,7},{5,4},{6,5},{7,6},{8,11},{9,8},{10,9... | collective-permute-start | bytes 1548296 | tf_op jit(solution)/shard_map/ppermute | solution.py:195
  66.8 21.8 %collective-permute-start.15 = (bf16[48,5120]{1,0:T(8,128)(2,1)S(1)}, bf16[48,5120]{1,0:T(8,128)(2,1)S(1)}, u32[]{:S(2)}, u32[]{:S(2)}) collective-permute-start(bf16[48,5120]{1,0:T(8,128)(2,1)S(1)} %bitcast.35), channel_id=1, source_target_pairs={{0,3},{1,0},{2,1},{3,2},{4,7},{5,4},{6,5},{7,6},{8,11},{9,8},{10,9... | collective-permute-start | bytes 1474568 | tf_op jit(solution)/shard_map/ppermute | solution.py:195
  88.6 24.9 %collective-permute-start.14 = (bf16[48,5120]{1,0:T(8,128)(2,1)S(1)}, bf16[48,5120]{1,0:T(8,128)(2,1)S(1)}, u32[]{:S(2)}, u32[]{:S(2)}) collective-permute-start(bf16[48,5120]{1,0:T(8,128)(2,1)S(1)} %bitcast.33), channel_id=1, source_target_pairs={{0,3},{1,0},{2,1},{3,2},{4,7},{5,4},{6,5},{7,6},{8,11},{9,8},{10,9... | collective-permute-start | bytes 1474568 | tf_op jit(solution)/shard_map/ppermute | solution.py:195
  91.4 22.2 %collective-permute-start.13 = (bf16[48,5120]{1,0:T(8,128)(2,1)S(1)}, bf16[48,5120]{1,0:T(8,128)(2,1)S(1)}, u32[]{:S(2)}, u32[]{:S(2)}) collective-permute-start(bf16[48,5120]{1,0:T(8,128)(2,1)S(1)} %bitcast.36), channel_id=1, source_target_pairs={{0,1},{1,2},{2,3},{3,0},{4,5},{5,6},{6,7},{7,4},{8,9},{9,10},{10,1... | collective-permute-start | bytes 1474568 | tf_op jit(solution)/shard_map/ppermute | solution.py:195
  91.4 23.2 %collective-permute-start.16 = (bf16[48,5120]{1,0:T(8,128)(2,1)S(1)}, bf16[48,5120]{1,0:T(8,128)(2,1)S(1)}, u32[]{:S(2)}, u32[]{:S(2)}) collective-permute-start(bf16[48,5120]{1,0:T(8,128)(2,1)S(1)} %collective-permute-done.12.refs_2_), channel_id=1, source_target_pairs={{0,1},{1,2},{2,3},{3,0},{4,5},{5,6},{6,7},{7,4},{8,9},{9,10},{10,1... | collective-permute-start | bytes 1474568 | tf_op jit(solution)/shard_map/ppermute | solution.py:195
  91.5 24.8 %collective-permute-start.17 = (bf16[48,5120]{1,0:T(8,128)(2,1)S(1)}, bf16[48,5120]{1,0:T(8,128)(2,1)S(1)}, u32[]{:S(2)}, u32[]{:S(2)}) collective-permute-start(bf16[48,5120]{1,0:T(8,128)(2,1)S(1)} %collective-permute-done.15.refs_5_), channel_id=1, source_target_pairs={{0,3},{1,0},{2,1},{3,2},{4,7},{5,4},{6,5},{7,6},{8,11},{9,8},{10,9... | collective-permute-start | bytes 1474568 | tf_op jit(solution)/shard_map/ppermute | solution.py:195
  112.1 45.4 %collective-permute-start.8 = (bf16[48,5120]{1,0:T(8,128)(2,1)S(1)}, bf16[48,5120]{1,0:T(8,128)(2,1)S(1)}, u32[]{:S(2)}, u32[]{:S(2)}) collective-permute-start(bf16[48,5120]{1,0:T(8,128)(2,1)S(1)} %slice.66), channel_id=1, source_target_pairs={{0,3},{1,0},{2,1},{3,2},{4,7},{5,4},{6,5},{7,6},{8,11},{9,8},{10,9... | collective-permute-start | bytes 1474568 | tf_op jit(solution)/shard_map/ppermute | solution.py:195
  113.4 44.1 %collective-permute-start.9 = (bf16[48,5120]{1,0:T(8,128)(2,1)S(1)}, bf16[48,5120]{1,0:T(8,128)(2,1)S(1)}, u32[]{:S(2)}, u32[]{:S(2)}) collective-permute-start(bf16[48,5120]{1,0:T(8,128)(2,1)S(1)} %slice.68), channel_id=1, source_target_pairs={{0,1},{1,2},{2,3},{3,0},{4,5},{5,6},{6,7},{7,4},{8,9},{9,10},{10,1... | collective-permute-start | bytes 1474568 | tf_op jit(solution)/shard_map/ppermute | solution.py:195
  113.7 21.8 %collective-permute-start.6 = (bf16[48,5120]{1,0:T(8,128)(2,1)S(1)}, bf16[48,5120]{1,0:T(8,128)(2,1)S(1)}, u32[]{:S(2)}, u32[]{:S(2)}) collective-permute-start(bf16[48,5120]{1,0:T(8,128)(2,1)S(1)} %get-tuple-element.22), channel_id=1, source_target_pairs={{0,1},{1,2},{2,3},{3,0},{4,5},{5,6},{6,7},{7,4},{8,9},{9,10},{10,1... | collective-permute-start | bytes 1474568 | tf_op jit(solution)/shard_map/ppermute | solution.py:195
  114.6 21.2 %collective-permute-start.10 = (bf16[48,5120]{1,0:T(8,128)(2,1)S(1)}, bf16[48,5120]{1,0:T(8,128)(2,1)S(1)}, u32[]{:S(2)}, u32[]{:S(2)}) collective-permute-start(bf16[48,5120]{1,0:T(8,128)(2,1)S(1)} %get-tuple-element.24), channel_id=1, source_target_pairs={{0,3},{1,0},{2,1},{3,2},{4,7},{5,4},{6,5},{7,6},{8,11},{9,8},{10,9... | collective-permute-start | bytes 1474568 | tf_op jit(solution)/shard_map/ppermute | solution.py:195
  134.1 44.8 %collective-permute-start.20 = (bf16[48,5120]{1,0:T(8,128)(2,1)S(1)}, bf16[48,5120]{1,0:T(8,128)(2,1)S(1)}, u32[]{:S(2)}, u32[]{:S(2)}) collective-permute-start(bf16[48,5120]{1,0:T(8,128)(2,1)S(1)} %slice.76), channel_id=1, source_target_pairs={{0,3},{1,0},{2,1},{3,2},{4,7},{5,4},{6,5},{7,6},{8,11},{9,8},{10,9... | collective-permute-start | bytes 1474568 | tf_op jit(solution)/shard_map/ppermute | solution.py:195
  135.5 10.5 %collective-permute-start.18 = (bf16[48,5120]{1,0:T(8,128)(2,1)S(1)}, bf16[48,5120]{1,0:T(8,128)(2,1)S(1)}, u32[]{:S(2)}, u32[]{:S(2)}) collective-permute-start(bf16[48,5120]{1,0:T(8,128)(2,1)S(1)} %get-tuple-element.28), channel_id=1, source_target_pairs={{0,1},{1,2},{2,3},{3,0},{4,5},{5,6},{6,7},{7,4},{8,9},{9,10},{10,1... | collective-permute-start | bytes 1474568 | tf_op jit(solution)/shard_map/ppermute | solution.py:195
  135.8 18.7 %collective-permute-start.22 = (bf16[48,5120]{1,0:T(8,128)(2,1)S(1)}, bf16[48,5120]{1,0:T(8,128)(2,1)S(1)}, u32[]{:S(2)}, u32[]{:S(2)}) collective-permute-start(bf16[48,5120]{1,0:T(8,128)(2,1)S(1)} %get-tuple-element.30), channel_id=1, source_target_pairs={{0,3},{1,0},{2,1},{3,2},{4,7},{5,4},{6,5},{7,6},{8,11},{9,8},{10,9... | collective-permute-start | bytes 1474568 | tf_op jit(solution)/shard_map/ppermute | solution.py:195
  146.0 11.7 %collective-permute-start.7 = (bf16[48,5120]{1,0:T(8,128)(2,1)S(1)}, bf16[48,5120]{1,0:T(8,128)(2,1)S(1)}, u32[]{:S(2)}, u32[]{:S(2)}) collective-permute-start(bf16[48,5120]{1,0:T(8,128)(2,1)S(1)} %add_convert_fusion.7), channel_id=1, source_target_pairs={{0,1},{1,2},{2,3},{3,0},{4,5},{5,6},{6,7},{7,4},{8,9},{9,10},{10,1... | collective-permute-start | bytes 1474568 | tf_op jit(solution)/shard_map/ppermute | solution.py:195
  154.5 9.7 %collective-permute-start.11 = (bf16[48,5120]{1,0:T(8,128)(2,1)S(1)}, bf16[48,5120]{1,0:T(8,128)(2,1)S(1)}, u32[]{:S(2)}, u32[]{:S(2)}) collective-permute-start(bf16[48,5120]{1,0:T(8,128)(2,1)S(1)} %add_convert_fusion.5), channel_id=1, source_target_pairs={{0,3},{1,0},{2,1},{3,2},{4,7},{5,4},{6,5},{7,6},{8,11},{9,8},{10,9... | collective-permute-start | bytes 1474568 | tf_op jit(solution)/shard_map/ppermute | solution.py:195
  157.5 21.4 %collective-permute-start.21 = (bf16[48,5120]{1,0:T(8,128)(2,1)S(1)}, bf16[48,5120]{1,0:T(8,128)(2,1)}, u32[]{:S(2)}, u32[]{:S(2)}) collective-permute-start(bf16[48,5120]{1,0:T(8,128)(2,1)S(1)} %slice.78), channel_id=1, source_target_pairs={{0,1},{1,2},{2,3},{3,0},{4,5},{5,6},{6,7},{7,4},{8,9},{9,10},{10,1... | collective-permute-start | bytes 1474568 | tf_op jit(solution)/shard_map/ppermute | solution.py:195
  157.6 21.4 %collective-permute-start.19 = (bf16[48,5120]{1,0:T(8,128)(2,1)}, bf16[48,5120]{1,0:T(8,128)(2,1)}, u32[]{:S(2)}, u32[]{:S(2)}) collective-permute-start(bf16[48,5120]{1,0:T(8,128)(2,1)} %add_convert_fusion.3), channel_id=1, source_target_pairs={{0,1},{1,2},{2,3},{3,0},{4,5},{5,6},{6,7},{7,4},{8,9},{9,10},{10,1... | collective-permute-start | bytes 1474568 | tf_op jit(solution)/shard_map/ppermute | solution.py:195
  157.7 21.3 %collective-permute-start.23 = (bf16[48,5120]{1,0:T(8,128)(2,1)}, bf16[48,5120]{1,0:T(8,128)(2,1)}, u32[]{:S(2)}, u32[]{:S(2)}) collective-permute-start(bf16[48,5120]{1,0:T(8,128)(2,1)} %add_convert_fusion.1), channel_id=1, source_target_pairs={{0,3},{1,0},{2,1},{3,2},{4,7},{5,4},{6,5},{7,6},{8,11},{9,8},{10,9... | collective-permute-start | bytes 1474568 | tf_op jit(solution)/shard_map/ppermute | solution.py:195
  166.3 29.0 %all-to-all-start.1 = ((bf16[32,3,2,2560]{3,2,1,0:T(2,128)(2,1)}), bf16[32,3,2,2560]{3,2,1,0:T(2,128)(2,1)S(1)}, u32[]{:S(2)}, u32[]{:S(2)}) async-start(bf16[32,3,2,2560]{3,2,1,0:T(2,128)(2,1)} %reshape.25), calls=%async_computation.1 | async-start | bytes 1966080 | tf_op jit(solution)/shard_map/all_to_all | solution.py:201
  195.2 20.1 %all-to-all-start.3 = ((bf16[32,3,2,2560]{3,2,1,0:T(2,128)(2,1)}), bf16[32,3,2,2560]{3,2,1,0:T(2,128)(2,1)S(1)}, u32[]{:S(2)}, u32[]{:S(2)}) async-start(bf16[32,3,2,2560]{3,2,1,0:T(2,128)(2,1)} %reshape.28), calls=%async_computation.3 | async-start | bytes 1966080 | tf_op jit(solution)/shard_map/all_to_all | solution.py:201

commit v4 on v3

--- a/solution.py
+++ b/solution.py
@@ -216,9 +216,10 @@
     )
     half = groups[0].shape[0] // 2
     gathered = []
-    for sent in groups:
+    for g, sent in enumerate(groups):
         own = to_nodes(sent, nodes)
-        top, low = own[:half], own[half:]
+        used = up_weight.shape[1] + (LANES if g == 0 else 0)
+        top, low = own[:half, :used], own[half:, :used]
         right_top, left_low = shift(top, 1), shift(low, -1)
         right_low, left_top = shift(low, 1), shift(top, -1)
         far_a, far_b = shift(right_top, 1), shift(left_low, -1)

time: 218 us -> 218 us (level)
  transfers between devices with their start and end apart: 28 -> 28, of which waited for: 11 -> 10; matrix products, arithmetic and copies ran while one was open for 5% -> 5% of each run, Pallas kernels for 16% -> 16%
where the time goes in v4:
time: 218 us; the launch traced here: 217 us
  waiting for transfers between devices  105 us (48%)
  starting transfers between devices  59 us (27%)
  Pallas kernels  36.5 us (17%)
  local copies, waits for them, and re-layouts  10.7 us (5%)
  other arithmetic  4.19 us (2%)
    all_to_all x4, waiting for transfers between devices, to_nodes(): lax.all_to_all(pieces, 'node', split_axis=0, concat_axis=0, tiled=True)  57.2 us
    ppermute x24, waiting for transfers between devices, shift(): lax.ppermute(value, 'local', [(i, (i + by) % size) for i in range(size)])  48.2 us
    all_to_all x4, starting transfers between devices, to_nodes(): lax.all_to_all(pieces, 'node', split_axis=0, concat_axis=0, tiled=True)  30.7 us
    ppermute x24, starting transfers between devices, shift(): lax.ppermute(value, 'local', [(i, (i + by) % size) for i in range(size)])  28.2 us
    pallas_call x2, Pallas kernels, up_project(): pl.pallas_call(functools.partial(up_kernel, len(parts), len(gate_parts),...  18.8 us
    pallas_call x2, Pallas kernels, down_project(): pl.pallas_call(down_kernel, grid=(STEPS,), out_shape=[jax.ShapeDtypeStruc...  16.6 us
    reshape x4, local copies, waits for them, and re-layouts, to_nodes(): pieces = value.reshape(nodes, rows // nodes, 2, width // 2)  6.23 us
  transfers between devices with their start and end apart: 28, of which 10 were waited for; matrix products, arithmetic and copies ran while one was open for 5% of the time, Pallas kernels for 16%

profile of v4, /device:TPU:1, one launch (start us, length us, event | category | flops | bytes accessed | tf_op | source)
XLA Modules:
  0.0 217.5 jit_solution(15735241978548222489)
XLA Ops:
  0.0 1.1 copy-done
  1.1 0.7 copy-done.1
  1.8 0.7 copy-done.2
  2.5 0.7 copy-done.3
  3.1 1.2 select.1
  4.3 1.2 reshape.24
  5.6 9.4 %all-to-all-start = ((bf16[32,3,2,2688]{3,2,1,0:T(2,128)(2,1)}), bf16[32,3,2,2688]{3,2,1,0:T(2,128)(2,1)S(1)}, u32[]{:S(2)}, u32[]{:S(2)}) async-start(bf16[32,3,2,2688]{3,2,1,0:T(2,128)(2,1)} %reshape.24), calls=%async_computation | async-start | bytes 2064384 | tf_op jit(solution)/shard_map/all_to_all | solution.py:201
  15.0 1.7 reshape.28
  16.7 15.1 %all-to-all-done = bf16[32,3,2,2688]{3,2,1,0:T(2,128)(2,1)S(1)} async-done(((bf16[32,3,2,2688]{3,2,1,0:T(2,128)(2,1)}), bf16[32,3,2,2688]{3,2,1,0:T(2,128)(2,1)S(1)}, u32[]{:S(2)}, u32[]{:S(2)}) %all-to-all-start) | async-done | bytes 1032224 | tf_op jit(solution)/shard_map/all_to_all | solution.py:201
  31.7 3.9 %all-to-all-start.2 = ((bf16[32,3,2,2560]{3,2,1,0:T(2,128)(2,1)}), bf16[32,3,2,2560]{3,2,1,0:T(2,128)(2,1)S(1)}, u32[]{:S(2)}, u32[]{:S(2)}) async-start(bf16[32,3,2,2560]{3,2,1,0:T(2,128)(2,1)} %reshape.28), calls=%async_computation.2 | async-start | bytes 1966080 | tf_op jit(solution)/shard_map/all_to_all | solution.py:201
  35.9 2.8 %collective-permute-start.3 = (bf16[48,5248]{1,0:T(8,128)(2,1)S(1)}, bf16[48,5248]{1,0:T(8,128)(2,1)S(1)}, u32[]{:S(2)}, u32[]{:S(2)}) collective-permute-start(bf16[48,5248]{1,0:T(8,128)(2,1)S(1)} %get-tuple-element.31.refs_1_.refs_9_), channel_id=1, source_target_pairs={{0,3},{1,0},{2,1},{3,2},{4,7},{5,4},{6,5},{7,6},{8,11},{9,8},{10,9... | collective-permute-start | bytes 1511432 | tf_op jit(solution)/shard_map/ppermute | solution.py:195
  38.7 13.2 %all-to-all-done.2 = bf16[32,3,2,2560]{3,2,1,0:T(2,128)(2,1)S(1)} async-done(((bf16[32,3,2,2560]{3,2,1,0:T(2,128)(2,1)}), bf16[32,3,2,2560]{3,2,1,0:T(2,128)(2,1)S(1)}, u32[]{:S(2)}, u32[]{:S(2)}) %all-to-all-start.2) | async-done | bytes 983072 | tf_op jit(solution)/shard_map/all_to_all | solution.py:201
  51.9 0.7 fusion.5
  52.6 1.4 collective-permute-start.12
  54.0 1.3 collective-permute-start.1
  55.3 1.4 collective-permute-start.2
  56.7 0.3 collective-permute-start.5
  57.0 1.2 collective-permute-start.4
  58.2 8.6 %collective-permute-done.12.refs_2_ = bf16[48,5120]{1,0:T(8,128)(2,1)S(1)} collective-permute-done((bf16[48,5120]{1,0:T(8,128)(2,1)S(1)}, bf16[48,5120]{1,0:T(8,128)(2,1)S(1)}, u32[]{:S(2)}, u32[]{:S(2)}) %collective-permute-start.12) | collective-permute-done | bytes 491552 | tf_op jit(solution)/shard_map/ppermute | solution.py:195
  66.8 1.4 collective-permute-start.15
  68.2 20.9 %collective-permute-done.15.refs_5_ = bf16[48,5120]{1,0:T(8,128)(2,1)S(1)} collective-permute-done((bf16[48,5120]{1,0:T(8,128)(2,1)S(1)}, bf16[48,5120]{1,0:T(8,128)(2,1)S(1)}, u32[]{:S(2)}, u32[]{:S(2)}) %collective-permute-start.15) | collective-permute-done | bytes 491552 | tf_op jit(solution)/shard_map/ppermute | solution.py:195
  89.0 2.6 %collective-permute-start.14 = (bf16[48,5120]{1,0:T(8,128)(2,1)S(1)}, bf16[48,5120]{1,0:T(8,128)(2,1)S(1)}, u32[]{:S(2)}, u32[]{:S(2)}) collective-permute-start(bf16[48,5120]{1,0:T(8,128)(2,1)S(1)} %bitcast.20), channel_id=1, source_target_pairs={{0,3},{1,0},{2,1},{3,2},{4,7},{5,4},{6,5},{7,6},{8,11},{9,8},{10,9... | collective-permute-start | bytes 1474568 | tf_op jit(solution)/shard_map/ppermute | solution.py:195
  91.7 2.7 %collective-permute-start.17 = (bf16[48,5120]{1,0:T(8,128)(2,1)S(1)}, bf16[48,5120]{1,0:T(8,128)(2,1)S(1)}, u32[]{:S(2)}, u32[]{:S(2)}) collective-permute-start(bf16[48,5120]{1,0:T(8,128)(2,1)S(1)} %collective-permute-done.15.refs_5_), channel_id=1, source_target_pairs={{0,3},{1,0},{2,1},{3,2},{4,7},{5,4},{6,5},{7,6},{8,11},{9,8},{10,9... | collective-permute-start | bytes 1474568 | tf_op jit(solution)/shard_map/ppermute | solution.py:195
  94.4 9.4 %up.2.hid = bf16[384,1152]{1,0:T(8,128)(2,1)S(1)} custom-call(bf16[48,5248]{1,0:T(8,128)(2,1)S(1)} %get-tuple-element.32.refs_0_.refs_8_, bf16[48,5248]{1,0:T(8,128)(2,1)S(1)} %get-tuple-element.31.refs_1_.refs_9_, bf16[48,5248]{1,0:T(8,128)(2,1)S(1)} %collective-permute-done.refs_2_.refs_10_, bf16[48,5248]{1,0:T(8,128)(2,1)S(1)} %collective-permute-done.1.refs_3_.refs_11_, ...), custom_call_target="tpu_custom_call" | custom-call | flops 4529848320 | bytes 16613376 | tf_op jit(solution)/shard_map/up/pallas_call | solution.py:149
  103.8 8.3 %down.4 = (bf16[96,5120]{1,0:T(8,128)(2,1)S(1)}, bf16[96,5120]{1,0:T(8,128)(2,1)S(1)}, bf16[96,5120]{1,0:T(8,128)(2,1)S(1)}, bf16[48,5120]{1,0:T(8,128)(2,1)S(1)}, bf16[48,5120]{1,0:T(8,128)(2,1)S(1)}) custom-call(bf16[384,1152]{1,0:T(8,128)(2,1)S(1)} %up.2.hid, bf16[3,384,5120]{2,1,0:T(8,128)(2,1)} %down.7), custom_call_target="tpu_custom_call" | custom-call | flops 4529848320 | bytes 16613376 | tf_op jit(solution)/shard_map/down/pallas_call | solution.py:178
  112.2 1.6 collective-permute-start.8
  114.0 0.4 collective-permute-done.16.refs_6_
  114.4 2.2 collective-permute-start.10
  116.6 9.4 %up.3.hid = bf16[384,1152]{1,0:T(8,128)(2,1)S(1)} custom-call(bf16[48,5120]{1,0:T(8,128)(2,1)S(1)} %bitcast.21, bf16[48,5120]{1,0:T(8,128)(2,1)S(1)} %bitcast.24, bf16[48,5120]{1,0:T(8,128)(2,1)S(1)} %collective-permute-done.12.refs_2_, bf16[48,5120]{1,0:T(8,128)(2,1)S(1)} %collective-permute-done.13.refs_3_, ...), custom_call_target="tpu_custom_call" | custom-call | flops 4529848320 | bytes 16613376 | tf_op jit(solution)/shard_map/up/pallas_call | solution.py:149
  126.0 8.3 %down.6 = (bf16[96,5120]{1,0:T(8,128)(2,1)S(1)}, bf16[96,5120]{1,0:T(8,128)(2,1)S(1)}, bf16[96,5120]{1,0:T(8,128)(2,1)S(1)}, bf16[48,5120]{1,0:T(8,128)(2,1)S(1)}, bf16[48,5120]{1,0:T(8,128)(2,1)S(1)}) custom-call(bf16[384,1152]{1,0:T(8,128)(2,1)S(1)} %up.3.hid, bf16[3,384,5120]{2,1,0:T(8,128)(2,1)} %down.7), custom_call_target="tpu_custom_call" | custom-call | flops 4529848320 | bytes 16613376 | tf_op jit(solution)/shard_map/down/pallas_call | solution.py:178
  134.3 1.5 collective-permute-start.20
  136.0 2.7 %collective-permute-start.22 = (bf16[48,5120]{1,0:T(8,128)(2,1)S(1)}, bf16[48,5120]{1,0:T(8,128)(2,1)S(1)}, u32[]{:S(2)}, u32[]{:S(2)}) collective-permute-start(bf16[48,5120]{1,0:T(8,128)(2,1)S(1)} %get-tuple-element.30), channel_id=1, source_target_pairs={{0,3},{1,0},{2,1},{3,2},{4,7},{5,4},{6,5},{7,6},{8,11},{9,8},{10,9... | collective-permute-start | bytes 1474568 | tf_op jit(solution)/shard_map/ppermute | solution.py:195
  138.8 7.0 %collective-permute-done.18 = bf16[48,5120]{1,0:T(8,128)(2,1)S(1)} collective-permute-done((bf16[48,5120]{1,0:T(8,128)(2,1)S(1)}, bf16[48,5120]{1,0:T(8,128)(2,1)S(1)}, u32[]{:S(2)}, u32[]{:S(2)}) %collective-permute-start.18) | collective-permute-done | bytes 491552 | tf_op jit(solution)/shard_map/ppermute | solution.py:195
  145.8 0.9 add_convert_fusion.3
  146.7 7.6 %collective-permute-done.22 = bf16[48,5120]{1,0:T(8,128)(2,1)S(1)} collective-permute-done((bf16[48,5120]{1,0:T(8,128)(2,1)S(1)}, bf16[48,5120]{1,0:T(8,128)(2,1)S(1)}, u32[]{:S(2)}, u32[]{:S(2)}) %collective-permute-start.22) | collective-permute-done | bytes 491552 | tf_op jit(solution)/shard_map/ppermute | solution.py:195
  154.3 2.3 %collective-permute-start.11 = (bf16[48,5120]{1,0:T(8,128)(2,1)S(1)}, bf16[48,5120]{1,0:T(8,128)(2,1)S(1)}, u32[]{:S(2)}, u32[]{:S(2)}) collective-permute-start(bf16[48,5120]{1,0:T(8,128)(2,1)S(1)} %add_convert_fusion.5), channel_id=1, source_target_pairs={{0,3},{1,0},{2,1},{3,2},{4,7},{5,4},{6,5},{7,6},{8,11},{9,8},{10,9... | collective-permute-start | bytes 1474568 | tf_op jit(solution)/shard_map/ppermute | solution.py:195
  156.6 0.9 add_convert_fusion.1
  157.6 2.7 %collective-permute-start.23 = (bf16[48,5120]{1,0:T(8,128)(2,1)}, bf16[48,5120]{1,0:T(8,128)(2,1)}, u32[]{:S(2)}, u32[]{:S(2)}) collective-permute-start(bf16[48,5120]{1,0:T(8,128)(2,1)} %add_convert_fusion.1), channel_id=1, source_target_pairs={{0,3},{1,0},{2,1},{3,2},{4,7},{5,4},{6,5},{7,6},{8,11},{9,8},{10,9... | collective-permute-start | bytes 1474568 | tf_op jit(solution)/shard_map/ppermute | solution.py:195
  160.3 3.7 %collective-permute-done.11 = bf16[48,5120]{1,0:T(8,128)(2,1)S(1)} collective-permute-done((bf16[48,5120]{1,0:T(8,128)(2,1)S(1)}, bf16[48,5120]{1,0:T(8,128)(2,1)S(1)}, u32[]{:S(2)}, u32[]{:S(2)}) %collective-permute-start.11) | collective-permute-done | bytes 491552 | tf_op jit(solution)/shard_map/ppermute | solution.py:195
  164.0 0.4 add_convert_fusion.6
  164.4 1.7 reshape.26
  166.1 13.5 %all-to-all-start.1 = ((bf16[32,3,2,2560]{3,2,1,0:T(2,128)(2,1)}), bf16[32,3,2,2560]{3,2,1,0:T(2,128)(2,1)S(1)}, u32[]{:S(2)}, u32[]{:S(2)}) async-start(bf16[32,3,2,2560]{3,2,1,0:T(2,128)(2,1)} %reshape.26), calls=%async_computation.1 | async-start | bytes 1966080 | tf_op jit(solution)/shard_map/all_to_all | solution.py:201
  179.6 1.7 add_convert_fusion.2
  181.4 1.7 reshape.29
  183.0 12.9 %all-to-all-done.1 = bf16[32,3,2,2560]{3,2,1,0:T(2,128)(2,1)S(1)} async-done(((bf16[32,3,2,2560]{3,2,1,0:T(2,128)(2,1)}), bf16[32,3,2,2560]{3,2,1,0:T(2,128)(2,1)S(1)}, u32[]{:S(2)}, u32[]{:S(2)}) %all-to-all-start.1) | async-done | bytes 983072 | tf_op jit(solution)/shard_map/all_to_all | solution.py:201
  195.9 3.9 %all-to-all-start.3 = ((bf16[32,3,2,2560]{3,2,1,0:T(2,128)(2,1)}), bf16[32,3,2,2560]{3,2,1,0:T(2,128)(2,1)S(1)}, u32[]{:S(2)}, u32[]{:S(2)}) async-start(bf16[32,3,2,2560]{3,2,1,0:T(2,128)(2,1)} %reshape.29), calls=%async_computation.3 | async-start | bytes 1966080 | tf_op jit(solution)/shard_map/all_to_all | solution.py:201
  199.9 16.1 %all-to-all-done.3 = bf16[32,3,2,2560]{3,2,1,0:T(2,128)(2,1)S(1)} async-done(((bf16[32,3,2,2560]{3,2,1,0:T(2,128)(2,1)}), bf16[32,3,2,2560]{3,2,1,0:T(2,128)(2,1)S(1)}, u32[]{:S(2)}, u32[]{:S(2)}) %all-to-all-start.3) | async-done | bytes 983072 | tf_op jit(solution)/shard_map/all_to_all | solution.py:201
  216.1 1.4 convolution_convert_fusion
  (45 shorter events, 1.5 us)
Async XLA Ops:
  0.0 1.1 copy-start
  1.1 0.7 copy-start.1
  1.8 0.7 copy-start.2
  2.5 0.7 copy-start.3
  5.6 26.2 %all-to-all-start = ((bf16[32,3,2,2688]{3,2,1,0:T(2,128)(2,1)}), bf16[32,3,2,2688]{3,2,1,0:T(2,128)(2,1)S(1)}, u32[]{:S(2)}, u32[]{:S(2)}) async-start(bf16[32,3,2,2688]{3,2,1,0:T(2,128)(2,1)} %reshape.24), calls=%async_computation | async-start | bytes 2064384 | tf_op jit(solution)/shard_map/all_to_all | solution.py:201
  31.7 20.2 %all-to-all-start.2 = ((bf16[32,3,2,2560]{3,2,1,0:T(2,128)(2,1)}), bf16[32,3,2,2560]{3,2,1,0:T(2,128)(2,1)S(1)}, u32[]{:S(2)}, u32[]{:S(2)}) async-start(bf16[32,3,2,2560]{3,2,1,0:T(2,128)(2,1)} %reshape.28), calls=%async_computation.2 | async-start | bytes 1966080 | tf_op jit(solution)/shard_map/all_to_all | solution.py:201
  35.9 20.8 %collective-permute-start.3 = (bf16[48,5248]{1,0:T(8,128)(2,1)S(1)}, bf16[48,5248]{1,0:T(8,128)(2,1)S(1)}, u32[]{:S(2)}, u32[]{:S(2)}) collective-permute-start(bf16[48,5248]{1,0:T(8,128)(2,1)S(1)} %get-tuple-element.31.refs_1_.refs_9_), channel_id=1, source_target_pairs={{0,3},{1,0},{2,1},{3,2},{4,7},{5,4},{6,5},{7,6},{8,11},{9,8},{10,9... | collective-permute-start | bytes 1511432 | tf_op jit(solution)/shard_map/ppermute | solution.py:195
  38.7 18.3 %collective-permute-start = (bf16[48,5248]{1,0:T(8,128)(2,1)S(1)}, bf16[48,5248]{1,0:T(8,128)(2,1)S(1)}, u32[]{:S(2)}, u32[]{:S(2)}) collective-permute-start(bf16[48,5248]{1,0:T(8,128)(2,1)S(1)} %get-tuple-element.32.refs_0_.refs_8_), channel_id=1, source_target_pairs={{0,1},{1,2},{2,3},{3,0},{4,5},{5,6},{6,7},{7,4},{8,9},{9,10},{10,1... | collective-permute-start | bytes 1511432 | tf_op jit(solution)/shard_map/ppermute | solution.py:195
  52.6 14.1 %collective-permute-start.12 = (bf16[48,5120]{1,0:T(8,128)(2,1)S(1)}, bf16[48,5120]{1,0:T(8,128)(2,1)S(1)}, u32[]{:S(2)}, u32[]{:S(2)}) collective-permute-start(bf16[48,5120]{1,0:T(8,128)(2,1)S(1)} %bitcast.19), channel_id=1, source_target_pairs={{0,1},{1,2},{2,3},{3,0},{4,5},{5,6},{6,7},{7,4},{8,9},{9,10},{10,1... | collective-permute-start | bytes 1474568 | tf_op jit(solution)/shard_map/ppermute | solution.py:195
  54.0 37.6 %collective-permute-start.1 = (bf16[48,5248]{1,0:T(8,128)(2,1)S(1)}, bf16[48,5248]{1,0:T(8,128)(2,1)S(1)}, u32[]{:S(2)}, u32[]{:S(2)}) collective-permute-start(bf16[48,5248]{1,0:T(8,128)(2,1)S(1)} %get-tuple-element.31.refs_1_.refs_9_), channel_id=1, source_target_pairs={{0,1},{1,2},{2,3},{3,0},{4,5},{5,6},{6,7},{7,4},{8,9},{9,10},{10,1... | collective-permute-start | bytes 1511432 | tf_op jit(solution)/shard_map/ppermute | solution.py:195
  55.3 36.3 %collective-permute-start.2 = (bf16[48,5248]{1,0:T(8,128)(2,1)S(1)}, bf16[48,5248]{1,0:T(8,128)(2,1)S(1)}, u32[]{:S(2)}, u32[]{:S(2)}) collective-permute-start(bf16[48,5248]{1,0:T(8,128)(2,1)S(1)} %get-tuple-element.32.refs_0_.refs_8_), channel_id=1, source_target_pairs={{0,3},{1,0},{2,1},{3,2},{4,7},{5,4},{6,5},{7,6},{8,11},{9,8},{10,9... | collective-permute-start | bytes 1511432 | tf_op jit(solution)/shard_map/ppermute | solution.py:195
  56.7 35.1 %collective-permute-start.5 = (bf16[48,5248]{1,0:T(8,128)(2,1)S(1)}, bf16[48,5248]{1,0:T(8,128)(2,1)S(1)}, u32[]{:S(2)}, u32[]{:S(2)}) collective-permute-start(bf16[48,5248]{1,0:T(8,128)(2,1)S(1)} %collective-permute-done.3.refs_5_.refs_13_), channel_id=1, source_target_pairs={{0,3},{1,0},{2,1},{3,2},{4,7},{5,4},{6,5},{7,6},{8,11},{9,8},{10,9... | collective-permute-start | bytes 1511432 | tf_op jit(solution)/shard_map/ppermute | solution.py:195
  57.0 37.4 %collective-permute-start.4 = (bf16[48,5248]{1,0:T(8,128)(2,1)S(1)}, bf16[48,5248]{1,0:T(8,128)(2,1)S(1)}, u32[]{:S(2)}, u32[]{:S(2)}) collective-permute-start(bf16[48,5248]{1,0:T(8,128)(2,1)S(1)} %collective-permute-done.refs_2_.refs_10_), channel_id=1, source_target_pairs={{0,1},{1,2},{2,3},{3,0},{4,5},{5,6},{6,7},{7,4},{8,9},{9,10},{10,1... | collective-permute-start | bytes 1511432 | tf_op jit(solution)/shard_map/ppermute | solution.py:195
  66.8 22.3 %collective-permute-start.15 = (bf16[48,5120]{1,0:T(8,128)(2,1)S(1)}, bf16[48,5120]{1,0:T(8,128)(2,1)S(1)}, u32[]{:S(2)}, u32[]{:S(2)}) collective-permute-start(bf16[48,5120]{1,0:T(8,128)(2,1)S(1)} %bitcast.22), channel_id=1, source_target_pairs={{0,3},{1,0},{2,1},{3,2},{4,7},{5,4},{6,5},{7,6},{8,11},{9,8},{10,9... | collective-permute-start | bytes 1474568 | tf_op jit(solution)/shard_map/ppermute | solution.py:195
  89.0 24.8 %collective-permute-start.14 = (bf16[48,5120]{1,0:T(8,128)(2,1)S(1)}, bf16[48,5120]{1,0:T(8,128)(2,1)S(1)}, u32[]{:S(2)}, u32[]{:S(2)}) collective-permute-start(bf16[48,5120]{1,0:T(8,128)(2,1)S(1)} %bitcast.20), channel_id=1, source_target_pairs={{0,3},{1,0},{2,1},{3,2},{4,7},{5,4},{6,5},{7,6},{8,11},{9,8},{10,9... | collective-permute-start | bytes 1474568 | tf_op jit(solution)/shard_map/ppermute | solution.py:195
  91.6 22.3 %collective-permute-start.13 = (bf16[48,5120]{1,0:T(8,128)(2,1)S(1)}, bf16[48,5120]{1,0:T(8,128)(2,1)S(1)}, u32[]{:S(2)}, u32[]{:S(2)}) collective-permute-start(bf16[48,5120]{1,0:T(8,128)(2,1)S(1)} %bitcast.23), channel_id=1, source_target_pairs={{0,1},{1,2},{2,3},{3,0},{4,5},{5,6},{6,7},{7,4},{8,9},{9,10},{10,1... | collective-permute-start | bytes 1474568 | tf_op jit(solution)/shard_map/ppermute | solution.py:195
  91.6 22.8 %collective-permute-start.16 = (bf16[48,5120]{1,0:T(8,128)(2,1)S(1)}, bf16[48,5120]{1,0:T(8,128)(2,1)S(1)}, u32[]{:S(2)}, u32[]{:S(2)}) collective-permute-start(bf16[48,5120]{1,0:T(8,128)(2,1)S(1)} %collective-permute-done.12.refs_2_), channel_id=1, source_target_pairs={{0,1},{1,2},{2,3},{3,0},{4,5},{5,6},{6,7},{7,4},{8,9},{9,10},{10,1... | collective-permute-start | bytes 1474568 | tf_op jit(solution)/shard_map/ppermute | solution.py:195
  91.7 24.8 %collective-permute-start.17 = (bf16[48,5120]{1,0:T(8,128)(2,1)S(1)}, bf16[48,5120]{1,0:T(8,128)(2,1)S(1)}, u32[]{:S(2)}, u32[]{:S(2)}) collective-permute-start(bf16[48,5120]{1,0:T(8,128)(2,1)S(1)} %collective-permute-done.15.refs_5_), channel_id=1, source_target_pairs={{0,3},{1,0},{2,1},{3,2},{4,7},{5,4},{6,5},{7,6},{8,11},{9,8},{10,9... | collective-permute-start | bytes 1474568 | tf_op jit(solution)/shard_map/ppermute | solution.py:195
  112.2 45.3 %collective-permute-start.8 = (bf16[48,5120]{1,0:T(8,128)(2,1)S(1)}, bf16[48,5120]{1,0:T(8,128)(2,1)S(1)}, u32[]{:S(2)}, u32[]{:S(2)}) collective-permute-start(bf16[48,5120]{1,0:T(8,128)(2,1)S(1)} %slice.58), channel_id=1, source_target_pairs={{0,3},{1,0},{2,1},{3,2},{4,7},{5,4},{6,5},{7,6},{8,11},{9,8},{10,9... | collective-permute-start | bytes 1474568 | tf_op jit(solution)/shard_map/ppermute | solution.py:195
  113.8 43.7 %collective-permute-start.9 = (bf16[48,5120]{1,0:T(8,128)(2,1)S(1)}, bf16[48,5120]{1,0:T(8,128)(2,1)S(1)}, u32[]{:S(2)}, u32[]{:S(2)}) collective-permute-start(bf16[48,5120]{1,0:T(8,128)(2,1)S(1)} %slice.60), channel_id=1, source_target_pairs={{0,1},{1,2},{2,3},{3,0},{4,5},{5,6},{6,7},{7,4},{8,9},{9,10},{10,1... | collective-permute-start | bytes 1474568 | tf_op jit(solution)/shard_map/ppermute | solution.py:195
  113.9 21.9 %collective-permute-start.6 = (bf16[48,5120]{1,0:T(8,128)(2,1)S(1)}, bf16[48,5120]{1,0:T(8,128)(2,1)S(1)}, u32[]{:S(2)}, u32[]{:S(2)}) collective-permute-start(bf16[48,5120]{1,0:T(8,128)(2,1)S(1)} %get-tuple-element.22), channel_id=1, source_target_pairs={{0,1},{1,2},{2,3},{3,0},{4,5},{5,6},{6,7},{7,4},{8,9},{9,10},{10,1... | collective-permute-start | bytes 1474568 | tf_op jit(solution)/shard_map/ppermute | solution.py:195
  114.4 21.6 %collective-permute-start.10 = (bf16[48,5120]{1,0:T(8,128)(2,1)S(1)}, bf16[48,5120]{1,0:T(8,128)(2,1)S(1)}, u32[]{:S(2)}, u32[]{:S(2)}) collective-permute-start(bf16[48,5120]{1,0:T(8,128)(2,1)S(1)} %get-tuple-element.24), channel_id=1, source_target_pairs={{0,3},{1,0},{2,1},{3,2},{4,7},{5,4},{6,5},{7,6},{8,11},{9,8},{10,9... | collective-permute-start | bytes 1474568 | tf_op jit(solution)/shard_map/ppermute | solution.py:195
  134.3 45.2 %collective-permute-start.20 = (bf16[48,5120]{1,0:T(8,128)(2,1)S(1)}, bf16[48,5120]{1,0:T(8,128)(2,1)S(1)}, u32[]{:S(2)}, u32[]{:S(2)}) collective-permute-start(bf16[48,5120]{1,0:T(8,128)(2,1)S(1)} %slice.68), channel_id=1, source_target_pairs={{0,3},{1,0},{2,1},{3,2},{4,7},{5,4},{6,5},{7,6},{8,11},{9,8},{10,9... | collective-permute-start | bytes 1474568 | tf_op jit(solution)/shard_map/ppermute | solution.py:195
  135.8 10.0 %collective-permute-start.18 = (bf16[48,5120]{1,0:T(8,128)(2,1)S(1)}, bf16[48,5120]{1,0:T(8,128)(2,1)S(1)}, u32[]{:S(2)}, u32[]{:S(2)}) collective-permute-start(bf16[48,5120]{1,0:T(8,128)(2,1)S(1)} %get-tuple-element.28), channel_id=1, source_target_pairs={{0,1},{1,2},{2,3},{3,0},{4,5},{5,6},{6,7},{7,4},{8,9},{9,10},{10,1... | collective-permute-start | bytes 1474568 | tf_op jit(solution)/shard_map/ppermute | solution.py:195
  136.0 18.3 %collective-permute-start.22 = (bf16[48,5120]{1,0:T(8,128)(2,1)S(1)}, bf16[48,5120]{1,0:T(8,128)(2,1)S(1)}, u32[]{:S(2)}, u32[]{:S(2)}) collective-permute-start(bf16[48,5120]{1,0:T(8,128)(2,1)S(1)} %get-tuple-element.30), channel_id=1, source_target_pairs={{0,3},{1,0},{2,1},{3,2},{4,7},{5,4},{6,5},{7,6},{8,11},{9,8},{10,9... | collective-permute-start | bytes 1474568 | tf_op jit(solution)/shard_map/ppermute | solution.py:195
  145.8 11.8 %collective-permute-start.7 = (bf16[48,5120]{1,0:T(8,128)(2,1)S(1)}, bf16[48,5120]{1,0:T(8,128)(2,1)S(1)}, u32[]{:S(2)}, u32[]{:S(2)}) collective-permute-start(bf16[48,5120]{1,0:T(8,128)(2,1)S(1)} %add_convert_fusion.7), channel_id=1, source_target_pairs={{0,1},{1,2},{2,3},{3,0},{4,5},{5,6},{6,7},{7,4},{8,9},{9,10},{10,1... | collective-permute-start | bytes 1474568 | tf_op jit(solution)/shard_map/ppermute | solution.py:195
  154.3 9.7 %collective-permute-start.11 = (bf16[48,5120]{1,0:T(8,128)(2,1)S(1)}, bf16[48,5120]{1,0:T(8,128)(2,1)S(1)}, u32[]{:S(2)}, u32[]{:S(2)}) collective-permute-start(bf16[48,5120]{1,0:T(8,128)(2,1)S(1)} %add_convert_fusion.5), channel_id=1, source_target_pairs={{0,3},{1,0},{2,1},{3,2},{4,7},{5,4},{6,5},{7,6},{8,11},{9,8},{10,9... | collective-permute-start | bytes 1474568 | tf_op jit(solution)/shard_map/ppermute | solution.py:195
  157.5 22.1 %collective-permute-start.21 = (bf16[48,5120]{1,0:T(8,128)(2,1)S(1)}, bf16[48,5120]{1,0:T(8,128)(2,1)}, u32[]{:S(2)}, u32[]{:S(2)}) collective-permute-start(bf16[48,5120]{1,0:T(8,128)(2,1)S(1)} %slice.70), channel_id=1, source_target_pairs={{0,1},{1,2},{2,3},{3,0},{4,5},{5,6},{6,7},{7,4},{8,9},{9,10},{10,1... | collective-permute-start | bytes 1474568 | tf_op jit(solution)/shard_map/ppermute | solution.py:195
  157.5 22.1 %collective-permute-start.19 = (bf16[48,5120]{1,0:T(8,128)(2,1)}, bf16[48,5120]{1,0:T(8,128)(2,1)}, u32[]{:S(2)}, u32[]{:S(2)}) collective-permute-start(bf16[48,5120]{1,0:T(8,128)(2,1)} %add_convert_fusion.3), channel_id=1, source_target_pairs={{0,1},{1,2},{2,3},{3,0},{4,5},{5,6},{6,7},{7,4},{8,9},{9,10},{10,1... | collective-permute-start | bytes 1474568 | tf_op jit(solution)/shard_map/ppermute | solution.py:195
  157.6 22.0 %collective-permute-start.23 = (bf16[48,5120]{1,0:T(8,128)(2,1)}, bf16[48,5120]{1,0:T(8,128)(2,1)}, u32[]{:S(2)}, u32[]{:S(2)}) collective-permute-start(bf16[48,5120]{1,0:T(8,128)(2,1)} %add_convert_fusion.1), channel_id=1, source_target_pairs={{0,3},{1,0},{2,1},{3,2},{4,7},{5,4},{6,5},{7,6},{8,11},{9,8},{10,9... | collective-permute-start | bytes 1474568 | tf_op jit(solution)/shard_map/ppermute | solution.py:195
  166.1 29.8 %all-to-all-start.1 = ((bf16[32,3,2,2560]{3,2,1,0:T(2,128)(2,1)}), bf16[32,3,2,2560]{3,2,1,0:T(2,128)(2,1)S(1)}, u32[]{:S(2)}, u32[]{:S(2)}) async-start(bf16[32,3,2,2560]{3,2,1,0:T(2,128)(2,1)} %reshape.26), calls=%async_computation.1 | async-start | bytes 1966080 | tf_op jit(solution)/shard_map/all_to_all | solution.py:201
  195.9 20.1 %all-to-all-start.3 = ((bf16[32,3,2,2560]{3,2,1,0:T(2,128)(2,1)}), bf16[32,3,2,2560]{3,2,1,0:T(2,128)(2,1)S(1)}, u32[]{:S(2)}, u32[]{:S(2)}) async-start(bf16[32,3,2,2560]{3,2,1,0:T(2,128)(2,1)} %reshape.29), calls=%async_computation.3 | async-start | bytes 1966080 | tf_op jit(solution)/shard_map/all_to_all | solution.py:201
